TPU v7x, 256 devices: a whole 4x4x8 slice. The times are simulated.
256 devices in a mesh: sx: 16 (over y, x), sy: 8 (over z), freq: 2 (over core).
Axes of the slice: x: 4, y: 4, z: 8, core: 2. Of those that a mesh axis runs over, the one named last changes fastest.
Arguments:
- update_basis: bfloat16 [4, 4096, 32, 1024], P('freq', ('sx', 'sy')), may hold values from -0.1875 to 0.1875
- update_coeff: bfloat16 [4, 4096, 32, 128], P('freq', ('sx', 'sy')), may hold values from -6 to 6
- owner: int32 [4096, 1], P(('sx', 'sy')), may hold values from 0 to 15; in each aligned block of 32 rows (0 to 31, 32 to 63, ...) at most 4 rows name the same one
- sep_rhs: bfloat16 [4, 16, 8, 1024, 128], P('freq', 'sx', 'sy'), may hold values from -6 to 6
- coupling: float32 [4, 16, 8, 4, 1024], P('freq', 'sx', 'sy'), may hold values from 0.1 to 0.25
- frontal_inverse: bfloat16 [4, 16, 8, 1024, 1024], P('freq', 'sx', 'sy'), may hold values from -0.2 to 1.2
Outputs:
- solution: float32 [4, 16, 8, 1024, 128], P('freq', 'sx', 'sy')
- residual_total: float32 [], replicated
Inputs may be any that keep to these rules, and one draw needn't show every extreme that they name: In the 32 children of one grid position no owner appears more than 4 times; in every draw some owner appears exactly 4 times at some position.
All inputs are finite; a program needn't handle non-finite values.
Results may differ from a plain program's by a relative error of at most 0.0019.
Values may be sent and summed in bfloat16 or wider, within the bound.
No kernel may reach another device: no remote copies, remote signals or barrier semaphores. Data moves between devices by JAX's collectives and lax.ppermute only.
A program may use at most 128 MiB of HBM per device.

v0:
```python
import functools

import jax
import jax.numpy as jnp
from jax import lax
from jax.sharding import Mesh
from jax.sharding import PartitionSpec as P

SWEEPS = 2
SX = ("sx_0", "sx_1")
SX_SY = ("sx_0", "sx_1", "sy")
SX_SY_FREQ = ("sx_0", "sx_1", "sy", "freq")


def extended(x, sides, width):
    edges = {}
    for axis, dim in sides:
        count, length = (lax.axis_size(axis), x.shape[dim])
        up = [(i, (i + 1) % count) for i in range(count - 1)]
        last = lax.slice_in_dim(x, length - width, length, axis=dim)
        initial = lax.slice_in_dim(x, 0, width, axis=dim)
        edges[dim] = (
            lax.ppermute(last, axis, up),
            lax.ppermute(initial, axis, [(b, a) for a, b in up]),
        )
    done = []
    for _, dim in sides:
        low, high = edges[dim]
        around = [(width, width) if d in done else (0, 0) for d in range(x.ndim)]
        x = jnp.concatenate([jnp.pad(low, around), x, jnp.pad(high, around)], axis=dim)
        done.append(dim)
    return x


def by_axis(x, axes):
    return functools.reduce(lax.psum, axes, x)


def on_device(update_basis, update_coeff, owner, sep_rhs, coupling, frontal_inverse):
    f_local = update_basis.shape[0]
    c_local = update_basis.shape[1]
    sep_size = update_basis.shape[3]
    rhs_count = update_coeff.shape[3]
    columns = lax.axis_size(SX)
    owners = owner[:, 0]
    capacity = max(2, 2 * c_local // columns)
    child_ids = jnp.arange(c_local, dtype=jnp.int32)
    same_owner = (owners[:, None] == owners[None, :]) & (child_ids[None, :] < child_ids[:, None])
    order_rank = jnp.sum(same_owner.astype(jnp.int32), axis=1)
    targets = owners * capacity + order_rank
    slot_ids = jnp.arange(columns * capacity, dtype=jnp.int32)
    slot_hits = slot_ids[:, None] == targets[None, :]
    source_child = jnp.sum(jnp.where(slot_hits, child_ids[None, :], 0), axis=1)
    is_filled = jnp.any(slot_hits, axis=1)
    basis_slots = jnp.take(update_basis, source_child, axis=1)
    coeff_taken = jnp.take(update_coeff, source_child, axis=1)
    coeff_slots = jnp.where(
        is_filled[None, :, None, None], coeff_taken, jnp.zeros((), jnp.bfloat16)
    )
    basis_piece = lax.all_to_all(basis_slots, SX, split_axis=1, concat_axis=1, tiled=True)
    coeff_piece = lax.all_to_all(coeff_slots, SX, split_axis=1, concat_axis=1, tiled=True)
    contribution = jnp.einsum(
        "fprs,fprn->fsn", basis_piece, coeff_piece, preferred_element_type=jnp.float32
    )
    right_side = sep_rhs[:, 0, 0].astype(jnp.float32) - contribution
    inverse_block = frontal_inverse[:, 0, 0]
    coupling_rows = coupling[:, 0, 0]

    def apply_inverse(field):
        return jnp.einsum(
            "fst,ftn->fsn",
            inverse_block,
            field.astype(jnp.bfloat16),
            preferred_element_type=jnp.float32,
        )

    solution = apply_inverse(right_side)
    residual = right_side
    for sweep_index in range(SWEEPS):
        padded = extended(
            solution[:, None, None].astype(jnp.bfloat16), ((SX, 1), ("sy", 2)), 1
        ).astype(jnp.float32)
        beside = coupling_rows[:, 0, :, None] * padded[:, 0, 1]
        beside = beside + coupling_rows[:, 1, :, None] * padded[:, 2, 1]
        beside = beside + coupling_rows[:, 2, :, None] * padded[:, 1, 0]
        beside = beside + coupling_rows[:, 3, :, None] * padded[:, 1, 2]
        residual = right_side - solution + beside
        solution = solution + apply_inverse(residual)
    freq_ids = lax.axis_index("freq") * f_local + jnp.arange(f_local, dtype=jnp.int32) + 1
    weights = freq_ids.astype(jnp.float32) ** 2
    local_sum = jnp.sum(weights * jnp.sum(residual * residual, axis=(1, 2)))
    weighted_sum = by_axis(local_sum, SX_SY_FREQ)
    entries = float(
        f_local * lax.axis_size("freq") * columns * lax.axis_size("sy") * sep_size * rhs_count
    )
    residual_total = jnp.sqrt(weighted_sum / entries + 1e-06)
    return (solution[:, None, None], residual_total)


def solution(mesh):
    finer = Mesh(
        mesh.devices.reshape(4, 4, mesh.shape["sy"], mesh.shape["freq"]),
        ("sx_0", "sx_1", "sy", "freq"),
    )
    return jax.shard_map(
        on_device,
        mesh=finer,
        in_specs=(
            P("freq", SX_SY, None, None),
            P("freq", SX_SY, None, None),
            P(SX_SY, None),
            P("freq", SX, "sy", None, None),
            P("freq", SX, "sy", None, None),
            P("freq", SX, "sy", None, None),
        ),
        out_specs=(P("freq", SX, "sy", None, None), P()),
        check_vma=False,
    )
```

profile of v0, /device:TPU:1, one launch (start us, length us, event | category | flops | bytes accessed | tf_op | source)
XLA Modules:
  0.0 236.0 jit_solution(9674063938604575623)
XLA Ops:
  0.6 0.0 copy-start
  0.6 0.9 convert_reduce_fusion
  1.6 0.7 multiply_add_fusion
  2.2 0.1 select_reduce_fusion
  2.3 0.1 fusion.59
  2.4 0.0 copy-done
  2.4 0.7 gather_fusion.1
  3.2 1.2 select_bitcast_fusion.1
  4.4 7.6 %all-to-all-start.1 = ((bf16[2,64,32,128]{3,2,0,1:T(8,128)(2,1)}), bf16[2,64,32,128]{3,2,0,1:T(8,128)(2,1)S(1)}, u32[]{:S(2)}, u32[]{:S(2)}) async-start(bf16[2,64,32,128]{3,2,0,1:T(8,128)(2,1)} %select_bitcast_fusion.1), calls=%async_computation.1 | async-start | bytes 2097152 | tf_op jit(solution)/shard_map/all_to_all | solution.py:61
  12.0 7.6 %gather_fusion = bf16[64,2,32,1024]{3,2,1,0:T(8,128)(2,1)} fusion(bf16[2,32,32,1024]{3,2,1,0:T(8,128)(2,1)} %param.6, s32[1024]{0:T(1024)S(1)} %pad_clamp_fusion), kind=kCustom, calls=%fused_computation | custom fusion | bytes 16777472 | tf_op jit(solution)/shard_map/jit(_take)/gather | solution.py:55
  19.6 7.5 %select_bitcast_fusion = bf16[2,64,32,1024]{3,2,0,1:T(8,128)(2,1)} fusion(bf16[64,2,32,1024]{3,2,1,0:T(8,128)(2,1)} %gather_fusion, pred[64]{0:T(512)(128)(4,1)S(1)} %compare_and_fusion), kind=kLoop, calls=%fused_computation.8 | loop fusion | flops 4194304 | bytes 16777280 | tf_op jit(solution)/shard_map/jit(_take)/select_n | solution.py:55
  27.0 0.0 copy-start.3
  27.0 1.0 all-to-all-done.1
  28.0 100.8 %all_to_all.10 = bf16[2,64,32,1024]{3,2,0,1:T(8,128)(2,1)S(1)} all-to-all(bf16[2,64,32,1024]{3,2,0,1:T(8,128)(2,1)} %select_bitcast_fusion), channel_id=1, replica_groups=mesh['sx_0'=4,'sx_1'=4,'sy'=8,'freq'=2] {'sx_0','sx_1'}, dimensions={1} | all-to-all | bytes 16777216 | tf_op jit(solution)/shard_map/all_to_all | solution.py:60
  128.8 0.0 copy-done.3
  128.8 0.0 copy-start.1
  128.8 3.5 %fusion.34 = f32[2,1024,128]{2,1,0:T(8,128)S(1)} fusion(bf16[2,64,32,1024]{3,2,0,1:T(8,128)(2,1)S(1)} %all_to_all.10, bf16[2,64,32,128]{3,2,0,1:T(8,128)(2,1)S(1)} %all-to-all-done.1, bf16[2,1,1,1024,128]{4,3,2,1,0:T(8,128)(2,1)S(1)} %copy-done.3), kind=kOutput, calls=%fused_computation.28 | convolution fusion | flops 1074266112 | bytes 11010048 | tf_op jit(solution)/shard_map/fprs,fprn->fsn/dot_general | solution.py:62
  132.3 0.0 copy-done.1
  132.3 1.3 fusion.31
  133.6 0.1 convert_bitcast_fusion.1
  133.6 1.3 collective-permute-start.3
  134.9 4.2 %collective-permute-start = (bf16[2,1,1,1024,128]{4,3,0,2,1:T(8,128)(2,1)S(1)}, bf16[2,1,1,1024,128]{4,3,0,2,1:T(8,128)(2,1)S(1)}, u32[]{:S(2)}, u32[]{:S(2)}) collective-permute-start(bf16[2,1,1,1024,128]{4,3,0,2,1:T(8,128)(2,1)S(1)} %convert_bitcast_fusion.1), channel_id=1, source_target_pairs={{0,2},{2,4},{4,6},{6,8},{8,10},{10,12},{12,14},{1,3},{3,5},{5,7},{... | collective-permute-start | bytes 1572872 | tf_op jit(solution)/shard_map/ppermute | solution.py:23
  139.2 1.3 collective-permute-start.2
  140.5 4.0 %collective-permute-start.1 = (bf16[2,1,1,1024,128]{4,3,0,2,1:T(8,128)(2,1)S(1)}, bf16[2,1,1,1024,128]{4,3,0,2,1:T(8,128)(2,1)S(1)}, u32[]{:S(2)}, u32[]{:S(2)}) collective-permute-start(bf16[2,1,1,1024,128]{4,3,0,2,1:T(8,128)(2,1)S(1)} %convert_bitcast_fusion.1), channel_id=1, source_target_pairs={{0,16},{16,32},{32,48},{48,64},{64,80},{80,96},{96,112},{112,128},... | collective-permute-start | bytes 1572872 | tf_op jit(solution)/shard_map/ppermute | solution.py:23
  144.5 0.0 copy-done.2
  144.6 2.4 %collective-permute-done.3 = bf16[2,1,1,1024,128]{4,3,0,2,1:T(8,128)(2,1)S(1)} collective-permute-done((bf16[2,1,1,1024,128]{4,3,0,2,1:T(8,128)(2,1)S(1)}, bf16[2,1,1,1024,128]{4,3,0,2,1:T(8,128)(2,1)S(1)}, u32[]{:S(2)}, u32[]{:S(2)}) %collective-permute-start.3) | collective-permute-done | bytes 524320 | tf_op jit(solution)/shard_map/ppermute | solution.py:24
  147.0 0.9 collective-permute-done
  147.9 3.9 %collective-permute-done.2 = bf16[2,1,1,1024,128]{4,3,0,2,1:T(8,128)(2,1)S(1)} collective-permute-done((bf16[2,1,1,1024,128]{4,3,0,2,1:T(8,128)(2,1)S(1)}, bf16[2,1,1,1024,128]{4,3,0,2,1:T(8,128)(2,1)S(1)}, u32[]{:S(2)}, u32[]{:S(2)}) %collective-permute-start.2) | collective-permute-done | bytes 524320 | tf_op jit(solution)/shard_map/ppermute | solution.py:24
  151.7 0.9 collective-permute-done.1
  152.7 0.7 fusion.6
  153.3 2.1 fusion.28
  155.4 0.1 convert_bitcast_fusion
  155.5 1.3 collective-permute-start.7
  156.8 5.0 %collective-permute-start.4 = (bf16[2,1,1,1024,128]{4,3,0,2,1:T(8,128)(2,1)S(1)}, bf16[2,1,1,1024,128]{4,3,0,2,1:T(8,128)(2,1)}, u32[]{:S(2)}, u32[]{:S(2)}) collective-permute-start(bf16[2,1,1,1024,128]{4,3,0,2,1:T(8,128)(2,1)S(1)} %convert_bitcast_fusion), channel_id=1, source_target_pairs={{0,2},{2,4},{4,6},{6,8},{8,10},{10,12},{12,14},{1,3},{3,5},{5,7},{... | collective-permute-start | bytes 1572872 | tf_op jit(solution)/shard_map/ppermute | solution.py:23
  161.8 1.3 collective-permute-start.6
  163.1 5.6 %collective-permute-start.5 = (bf16[2,1,1,1024,128]{4,3,0,2,1:T(8,128)(2,1)S(1)}, bf16[2,1,1,1024,128]{4,3,0,2,1:T(8,128)(2,1)}, u32[]{:S(2)}, u32[]{:S(2)}) collective-permute-start(bf16[2,1,1,1024,128]{4,3,0,2,1:T(8,128)(2,1)S(1)} %convert_bitcast_fusion), channel_id=1, source_target_pairs={{0,16},{16,32},{32,48},{48,64},{64,80},{80,96},{96,112},{112,128},... | collective-permute-start | bytes 1572872 | tf_op jit(solution)/shard_map/ppermute | solution.py:23
  168.6 0.0 collective-permute-done.7
  168.6 0.0 collective-permute-done.4
  168.6 5.3 %collective-permute-done.6 = bf16[2,1,1,1024,128]{4,3,0,2,1:T(8,128)(2,1)} collective-permute-done((bf16[2,1,1,1024,128]{4,3,0,2,1:T(8,128)(2,1)S(1)}, bf16[2,1,1,1024,128]{4,3,0,2,1:T(8,128)(2,1)}, u32[]{:S(2)}, u32[]{:S(2)}) %collective-permute-start.6) | collective-permute-done | bytes 524320 | tf_op jit(solution)/shard_map/ppermute | solution.py:24
  174.0 0.8 collective-permute-done.5
  174.8 2.7 %fusion.9 = f32[2,3,3,1024,128]{4,3,0,2,1:T(8,128)S(1)} fusion(bf16[2,1,1,1024,128]{4,3,0,2,1:T(8,128)(2,1)} %collective-permute-done.7, bf16[2,1,1,1024,128]{4,3,0,2,1:T(8,128)(2,1)} %collective-permute-done.4, bf16[2,1,1,1024,128]{4,3,0,2,1:T(8,128)(2,1)} %collective-permute-done.6, bf16[2,1,1,1024,128]{4,3,0,2,1:T(8,128)(2,1)S(1)} %convert_bitcast_fusion, ...), kind=kLoop, calls=%fused_computation.14 | loop fusion | flops 33030144 | bytes 12058624 | tf_op jit(solution)/shard_map/convert_element_type | solution.py:82
  177.5 1.7 multiply_reduce_fusion
  179.2 0.6 multiply_reduce_fusion.1
  179.8 13.2 %psum.28 = f32[]{:T(128)} all-reduce(f32[]{:T(128)} %multiply_reduce_fusion.1), channel_id=1, replica_groups=mesh['sx_0'=4,'sx_1'=4,'sy'=8,'freq'=2] {'sx_0'}, use_global_device_ids=true, to_apply=%region_5.6 | all-reduce | flops 1 | bytes 8 | tf_op jit(solution)/shard_map/psum | solution.py:36
  193.0 6.6 %psum.29 = f32[]{:T(128)} all-reduce(f32[]{:T(128)} %psum.28), channel_id=1, replica_groups=mesh['sx_0'=4,'sx_1'=4,'sy'=8,'freq'=2] {'sx_1'}, use_global_device_ids=true, to_apply=%region_6.7 | all-reduce | flops 1 | bytes 8 | tf_op jit(solution)/shard_map/psum | solution.py:36
  199.6 15.5 %psum.30 = f32[]{:T(128)} all-reduce(f32[]{:T(128)} %psum.29), channel_id=1, replica_groups=mesh['sx_0'=4,'sx_1'=4,'sy'=8,'freq'=2] {'sy'}, use_global_device_ids=true, to_apply=%region_7.8 | all-reduce | flops 1 | bytes 8 | tf_op jit(solution)/shard_map/psum | solution.py:36
  215.2 4.4 %fusion.22 = f32[2,1,1,1024,128]{4,3,2,1,0:T(8,128)} fusion(f32[2,1024,128]{2,1,0:T(8,128)S(1)} %fusion.28, bf16[2,1,1,1024,1024]{4,3,2,1,0:T(8,128)(2,1)} %param.11, bf16[2,1024,128]{2,1,0:T(8,128)(2,1)S(1)} %get-tuple-element.11), kind=kOutput, calls=%fused_computation.23 | convolution fusion | flops 537133056 | bytes 6815744 | tf_op jit(solution)/shard_map/fst,ftn->fsn/dot_general | solution.py:70
  219.6 14.7 %psum.31 = f32[]{:T(128)} all-reduce(f32[]{:T(128)} %psum.30), channel_id=1, replica_groups=mesh['sx_0'=4,'sx_1'=4,'sy'=8,'freq'=2] {'freq'}, use_global_device_ids=true, to_apply=%region_8.9 | all-reduce | flops 1 | bytes 8 | tf_op jit(solution)/shard_map/psum | solution.py:36
  (7 shorter events, 0.1 us)
Async XLA Ops:
  0.6 1.8 copy-start
  4.4 23.6 %all-to-all-start.1 = ((bf16[2,64,32,128]{3,2,0,1:T(8,128)(2,1)}), bf16[2,64,32,128]{3,2,0,1:T(8,128)(2,1)S(1)}, u32[]{:S(2)}, u32[]{:S(2)}) async-start(bf16[2,64,32,128]{3,2,0,1:T(8,128)(2,1)} %select_bitcast_fusion.1), calls=%async_computation.1 | async-start | bytes 2097152 | tf_op jit(solution)/shard_map/all_to_all | solution.py:61
  27.0 101.8 %copy-start.3 = (bf16[2,1,1,1024,128]{4,3,2,1,0:T(8,128)(2,1)S(1)}, bf16[2,1,1,1024,128]{4,3,2,1,0:T(8,128)(2,1)}, u32[]{:S(2)}) copy-start(bf16[2,1,1,1024,128]{4,3,2,1,0:T(8,128)(2,1)} %param.9) | copy-start | bytes 1572868
  128.8 3.5 %copy-start.1 = (bf16[2,1,1,1024,1024]{4,3,2,1,0:T(8,128)(2,1)S(1)}, bf16[2,1,1,1024,1024]{4,3,2,1,0:T(8,128)(2,1)}, u32[]{:S(2)}) copy-start(bf16[2,1,1,1024,1024]{4,3,2,1,0:T(8,128)(2,1)} %param.11) | copy-start | bytes 12582916
  128.8 15.7 %copy-start.2 = (f32[2,1,1,4,1024]{4,3,2,1,0:T(4,128)S(1)}, f32[2,1,1,4,1024]{4,3,2,1,0:T(4,128)}, u32[]{:S(2)}) copy-start(f32[2,1,1,4,1024]{4,3,2,1,0:T(4,128)} %param.10) | copy-start | bytes 98308
  133.6 13.3 %collective-permute-start.3 = (bf16[2,1,1,1024,128]{4,3,0,2,1:T(8,128)(2,1)S(1)}, bf16[2,1,1,1024,128]{4,3,0,2,1:T(8,128)(2,1)S(1)}, u32[]{:S(2)}, u32[]{:S(2)}) collective-permute-start(bf16[2,1,1,1024,128]{4,3,0,2,1:T(8,128)(2,1)S(1)} %convert_bitcast_fusion.1), channel_id=1, source_target_pairs={{2,0},{4,2},{6,4},{8,6},{10,8},{12,10},{14,12},{3,1},{5,3},{7,5},{... | collective-permute-start | bytes 1572872 | tf_op jit(solution)/shard_map/ppermute | solution.py:24
  134.9 12.9 %collective-permute-start = (bf16[2,1,1,1024,128]{4,3,0,2,1:T(8,128)(2,1)S(1)}, bf16[2,1,1,1024,128]{4,3,0,2,1:T(8,128)(2,1)S(1)}, u32[]{:S(2)}, u32[]{:S(2)}) collective-permute-start(bf16[2,1,1,1024,128]{4,3,0,2,1:T(8,128)(2,1)S(1)} %convert_bitcast_fusion.1), channel_id=1, source_target_pairs={{0,2},{2,4},{4,6},{6,8},{8,10},{10,12},{12,14},{1,3},{3,5},{5,7},{... | collective-permute-start | bytes 1572872 | tf_op jit(solution)/shard_map/ppermute | solution.py:23
  139.2 12.6 %collective-permute-start.2 = (bf16[2,1,1,1024,128]{4,3,0,2,1:T(8,128)(2,1)S(1)}, bf16[2,1,1,1024,128]{4,3,0,2,1:T(8,128)(2,1)S(1)}, u32[]{:S(2)}, u32[]{:S(2)}) collective-permute-start(bf16[2,1,1,1024,128]{4,3,0,2,1:T(8,128)(2,1)S(1)} %convert_bitcast_fusion.1), channel_id=1, source_target_pairs={{16,0},{32,16},{48,32},{64,48},{80,64},{96,80},{112,96},{128,112},... | collective-permute-start | bytes 1572872 | tf_op jit(solution)/shard_map/ppermute | solution.py:24
  140.5 12.2 %collective-permute-start.1 = (bf16[2,1,1,1024,128]{4,3,0,2,1:T(8,128)(2,1)S(1)}, bf16[2,1,1,1024,128]{4,3,0,2,1:T(8,128)(2,1)S(1)}, u32[]{:S(2)}, u32[]{:S(2)}) collective-permute-start(bf16[2,1,1,1024,128]{4,3,0,2,1:T(8,128)(2,1)S(1)} %convert_bitcast_fusion.1), channel_id=1, source_target_pairs={{0,16},{16,32},{32,48},{48,64},{64,80},{80,96},{96,112},{112,128},... | collective-permute-start | bytes 1572872 | tf_op jit(solution)/shard_map/ppermute | solution.py:23
  155.5 13.1 %collective-permute-start.7 = (bf16[2,1,1,1024,128]{4,3,0,2,1:T(8,128)(2,1)S(1)}, bf16[2,1,1,1024,128]{4,3,0,2,1:T(8,128)(2,1)}, u32[]{:S(2)}, u32[]{:S(2)}) collective-permute-start(bf16[2,1,1,1024,128]{4,3,0,2,1:T(8,128)(2,1)S(1)} %convert_bitcast_fusion), channel_id=1, source_target_pairs={{2,0},{4,2},{6,4},{8,6},{10,8},{12,10},{14,12},{3,1},{5,3},{7,5},{... | collective-permute-start | bytes 1572872 | tf_op jit(solution)/shard_map/ppermute | solution.py:24
  156.8 11.8 %collective-permute-start.4 = (bf16[2,1,1,1024,128]{4,3,0,2,1:T(8,128)(2,1)S(1)}, bf16[2,1,1,1024,128]{4,3,0,2,1:T(8,128)(2,1)}, u32[]{:S(2)}, u32[]{:S(2)}) collective-permute-start(bf16[2,1,1,1024,128]{4,3,0,2,1:T(8,128)(2,1)S(1)} %convert_bitcast_fusion), channel_id=1, source_target_pairs={{0,2},{2,4},{4,6},{6,8},{8,10},{10,12},{12,14},{1,3},{3,5},{5,7},{... | collective-permute-start | bytes 1572872 | tf_op jit(solution)/shard_map/ppermute | solution.py:23
  161.8 12.2 %collective-permute-start.6 = (bf16[2,1,1,1024,128]{4,3,0,2,1:T(8,128)(2,1)S(1)}, bf16[2,1,1,1024,128]{4,3,0,2,1:T(8,128)(2,1)}, u32[]{:S(2)}, u32[]{:S(2)}) collective-permute-start(bf16[2,1,1,1024,128]{4,3,0,2,1:T(8,128)(2,1)S(1)} %convert_bitcast_fusion), channel_id=1, source_target_pairs={{16,0},{32,16},{48,32},{64,48},{80,64},{96,80},{112,96},{128,112},... | collective-permute-start | bytes 1572872 | tf_op jit(solution)/shard_map/ppermute | solution.py:24
  163.1 11.7 %collective-permute-start.5 = (bf16[2,1,1,1024,128]{4,3,0,2,1:T(8,128)(2,1)S(1)}, bf16[2,1,1,1024,128]{4,3,0,2,1:T(8,128)(2,1)}, u32[]{:S(2)}, u32[]{:S(2)}) collective-permute-start(bf16[2,1,1,1024,128]{4,3,0,2,1:T(8,128)(2,1)S(1)} %convert_bitcast_fusion), channel_id=1, source_target_pairs={{0,16},{16,32},{32,48},{48,64},{64,80},{80,96},{96,112},{112,128},... | collective-permute-start | bytes 1572872 | tf_op jit(solution)/shard_map/ppermute | solution.py:23
where the time goes:
time: 237 us; the launch traced here: 236 us
  blocking collectives  151 us (64%)
  starting transfers between devices  31.5 us (13%)
  other arithmetic  16.3 us (7%)
  waiting for transfers between devices  15.2 us (6%)
  matrix products  11.3 us (5%)
  local copies, waits for them, and re-layouts  8.41 us (4%)
  between operations  2.63 us (1%)
    all_to_all x1, blocking collectives, on_device(): lax.all_to_all(basis_slots, SX, split_axis=1, concat_axis=1, tiled=True)  101 us
    psum x4, blocking collectives, by_axis(): return functools.reduce(lax.psum, axes, x)  50 us
    ppermute x4, starting transfers between devices, extended(): lax.ppermute(last, axis, up)  18.7 us
    ppermute x4, waiting for transfers between devices, extended(): lax.ppermute(initial, axis, [(b, a) for a, b in up])  11.6 us
    dot_general x3, matrix products, apply_inverse(): jnp.einsum('fst,ftn->fsn', inverse_block, field.astype(jnp.bfloat16), pre...  7.77 us
    gather x1, local copies, waits for them, and re-layouts, on_device(): basis_slots = jnp.take(update_basis, source_child, axis=1)  7.6 us
    all_to_all x1, starting transfers between devices, on_device(): lax.all_to_all(coeff_slots, SX, split_axis=1, concat_axis=1, tiled=True)  7.57 us
    select_n x2, other arithmetic, on_device(): basis_slots = jnp.take(update_basis, source_child, axis=1)  7.48 us
  transfers between devices with their start and end apart: 9, of which 7 were waited for; matrix products, arithmetic and copies ran while one was open for 6% of the time, Pallas kernels for 0%

commit v1 on v0

v1 whole, which is shorter than its diff:
```python
import functools

import jax
import jax.numpy as jnp
from jax import lax
from jax.experimental import pallas as pl
from jax.experimental.pallas import tpu as pltpu
from jax.sharding import Mesh
from jax.sharding import PartitionSpec as P

SWEEPS = 2
SIDE = 4
CAP = 4
ROWS = 256
SX = ("sx_0", "sx_1")
SX_SY = ("sx_0", "sx_1", "sy")
ORDER = (0, 1, 3, 2)


def products_kernel(plan, owner_ref, place_ref, basis_ref, coeff_ref, *rest):
    outs = rest[: len(plan)]
    slots, used, stacked, weights = rest[len(plan) :]
    children = owner_ref.shape[0]
    rank = basis_ref.shape[2]
    rhs_count = coeff_ref.shape[3]
    step = pl.program_id(0)

    @pl.when(step == 0)
    def _():
        for o in range(SIDE * SIDE):
            used[o] = 0
        for s in range(SIDE * SIDE * CAP):
            slots[s] = children

        def put(c, carry):
            o = owner_ref[c]
            k = used[o]
            slots[o * CAP + k] = c
            used[o] = k + 1
            return carry

        lax.fori_loop(0, children, put, 0)
        weights[...] = jnp.zeros_like(weights)

    first = 0
    for out, (f, ahead, pairs) in zip(outs, plan, strict=True):
        for n, pair in enumerate(pairs):

            @pl.when(step == first + n)
            def _(out=out, f=f, ahead=ahead, pair=pair):
                for b, beside in enumerate(pair):
                    offsets = (ahead, beside) if f == 0 else (beside, ahead)
                    row = lax.rem(place_ref[0] + offsets[0], SIDE)
                    column = lax.rem(place_ref[1] + offsets[1], SIDE)
                    o = row * SIDE + column
                    for k in range(CAP):
                        c = slots[o * CAP + k]
                        filled = c < children
                        c = jnp.where(filled, c, 0)
                        at = (b * CAP + k) * rank
                        stacked[at : at + rank, :] = basis_ref[f, c]
                        coeff = coeff_ref[f, c]
                        weights[at : at + rank, b * rhs_count : (b + 1) * rhs_count] = jnp.where(
                            filled, coeff, jnp.zeros_like(coeff)
                        )
                for r in range(0, stacked.shape[1], ROWS):
                    product = lax.dot_general(
                        stacked[:, r : r + ROWS],
                        weights[...],
                        (((0,), (0,)), ((), ())),
                        preferred_element_type=jnp.float32,
                    )
                    for b in range(2):
                        piece = product[:, b * rhs_count : (b + 1) * rhs_count]
                        out[b, r : r + ROWS, :] = piece.astype(out.dtype)

        first += len(pairs)


def owner_products(plan, dtypes, owners, place, basis, coeff):
    f_local, children, rank, sep_size = basis.shape
    rhs_count = coeff.shape[3]
    steps = sum(len(pairs) for _, _, pairs in plan)
    out_specs, out_shape, first = [], [], 0
    for (_, _, pairs), dtype in zip(plan, dtypes, strict=True):
        out_specs.append(
            pl.BlockSpec(
                (2, sep_size, rhs_count),
                lambda i, *_, first=first, n=len(pairs): (jnp.clip(i - first, 0, n - 1), 0, 0),
            )
        )
        out_shape.append(jax.ShapeDtypeStruct((2 * len(pairs), sep_size, rhs_count), dtype))
        first += len(pairs)
    return pl.pallas_call(
        functools.partial(products_kernel, plan),
        grid_spec=pltpu.PrefetchScalarGridSpec(
            num_scalar_prefetch=2,
            grid=(steps,),
            in_specs=[
                pl.BlockSpec((f_local, children, rank, sep_size), lambda i, *_: (0, 0, 0, 0)),
                pl.BlockSpec((f_local, children, rank, rhs_count), lambda i, *_: (0, 0, 0, 0)),
            ],
            out_specs=out_specs,
            scratch_shapes=[
                pltpu.SMEM((SIDE * SIDE * CAP,), jnp.int32),
                pltpu.SMEM((SIDE * SIDE,), jnp.int32),
                pltpu.VMEM((2 * CAP * rank, sep_size), jnp.bfloat16),
                pltpu.VMEM((2 * CAP * rank, 2 * rhs_count), jnp.bfloat16),
            ],
        ),
        out_shape=out_shape,
        cost_estimate=pl.CostEstimate(
            flops=2 * steps * 4 * CAP * rank * sep_size * rhs_count * 2,
            bytes_accessed=basis.size * 2 + steps * 2 * sep_size * rhs_count * 2,
            transcendentals=0,
        ),
    )(owners, place, basis, coeff)


def turn(x, axis, by):
    return lax.ppermute(x, axis, [(i, (i + by) % SIDE) for i in range(SIDE)])


def add_into(x, index, y):
    return x.at[index].add(y)


def packed(x, power):
    scaled = (x * jnp.exp2(power)).astype(jnp.float16)
    tail = jnp.broadcast_to(power.astype(jnp.float16), (16, x.shape[1]))
    return jnp.concatenate([scaled, tail])


def unpacked(y):
    rows = y.shape[0] - 16
    power = y[rows, 0].astype(jnp.float32)
    return (y[:rows].astype(jnp.float32) * jnp.exp2(-power), power)


def summed(x, axis):
    copies = jnp.broadcast_to(x, (lax.axis_size(axis), *x.shape))
    return jnp.sum(lax.all_to_all(copies, axis, 0, 0, tiled=True), axis=0)


def neighbours(x, axis, count):
    up = [(i, i + 1) for i in range(count - 1)]
    return (lax.ppermute(x, axis, up), lax.ppermute(x, axis, [(b, a) for a, b in up]))


def on_device(update_basis, update_coeff, owner, sep_rhs, coupling, frontal_inverse):
    f_local = update_basis.shape[0]
    sep_size = update_basis.shape[3]
    rhs_count = update_coeff.shape[3]
    columns = lax.axis_size(SX)
    place = jnp.stack([lax.axis_index("sx_0"), lax.axis_index("sx_1")]).astype(jnp.int32)
    owners = owner[:, 0]

    plan = tuple((f, 2, (pair,)) for f in range(2) for pair in ((0, 1), (3, 2)))
    far = owner_products(plan, (jnp.bfloat16,) * 4, owners, place, update_basis, update_coeff)
    plan = tuple((f, ahead, ((0, 1), (3, 2))) for f in range(2) for ahead in (1, 3, 0))
    dtypes = (jnp.bfloat16, jnp.bfloat16, jnp.float32) * 2
    near = owner_products(plan, dtypes, owners, place, update_basis, update_coeff)

    axes = (("sx_0", "sx_1"), ("sx_1", "sx_0"))
    half = sep_size // 2
    contribution = []
    got = [(turn(far[2 * f], axes[f][0], 1), turn(far[2 * f + 1], axes[f][0], -1)) for f in range(2)]
    sums = []
    for f in range(2):
        following, preceding, own = near[3 * f : 3 * f + 3]
        following = add_into(following, slice(0, 2), got[f][0])
        preceding = add_into(preceding, slice(2, 4), got[f][1])
        a = turn(following, axes[f][0], 1)
        b = turn(preceding, axes[f][0], -1)
        sums.append((a, b, own))
    for f in range(2):
        a, b, own = sums[f]
        total = [own[i] + a[i].astype(jnp.float32) + b[i].astype(jnp.float32) for i in range(4)]
        axis = axes[f][1]
        largest = functools.reduce(jnp.maximum, [jnp.max(jnp.abs(part)) for part in total[1:]])
        power = jnp.clip(14.0 - jnp.ceil(jnp.log2(largest)), -60.0, 100.0)
        a, a_power = unpacked(turn(packed(total[3][:half], power), axis, 1))
        b, b_power = unpacked(turn(packed(total[3][half:], power), axis, -1))
        following = jnp.concatenate([total[1][:half] + a, total[1][half:]])
        preceding = jnp.concatenate([total[2][:half], total[2][half:] + b])
        a, _ = unpacked(turn(packed(following, jnp.minimum(power, a_power)), axis, 1))
        b, _ = unpacked(turn(packed(preceding, jnp.minimum(power, b_power)), axis, -1))
        contribution.append(total[0] + a + b)
    contribution = jnp.stack(contribution)

    right_side = sep_rhs[:, 0, 0].astype(jnp.float32) - contribution
    inverse_block = frontal_inverse[:, 0, 0]
    coupling_rows = coupling[:, 0, 0]

    def apply_inverse(field):
        return jnp.einsum(
            "fst,ftn->fsn",
            inverse_block,
            field.astype(jnp.bfloat16),
            preferred_element_type=jnp.float32,
        )

    solution = apply_inverse(right_side)
    residual = right_side
    for _ in range(SWEEPS):
        sent = solution.astype(jnp.bfloat16)
        around = neighbours(sent, SX, columns) + neighbours(sent, "sy", lax.axis_size("sy"))
        residual = right_side - solution
        for d in range(4):
            residual = residual + coupling_rows[:, d, :, None] * around[d].astype(jnp.float32)
        solution = solution + apply_inverse(residual)
    freq_ids = lax.axis_index("freq") * f_local + jnp.arange(f_local, dtype=jnp.int32) + 1
    weights = freq_ids.astype(jnp.float32) ** 2
    weighted_sum = jnp.sum(weights * jnp.sum(residual * residual, axis=(1, 2)))
    spread = jnp.broadcast_to(weighted_sum, (8, rhs_count))
    spread = spread + lax.ppermute(spread, "freq", [(0, 1), (1, 0)])
    spread = summed(spread, "sy")
    weighted_sum = summed(spread, SX)[0, 0]
    entries = float(
        f_local * lax.axis_size("freq") * columns * lax.axis_size("sy") * sep_size * rhs_count
    )
    residual_total = jnp.sqrt(weighted_sum / entries + 1e-06)
    return (solution[:, None, None], residual_total)


def solution(mesh):
    finer = Mesh(
        mesh.devices.reshape(SIDE, SIDE, mesh.shape["sy"], mesh.shape["freq"]),
        ("sx_0", "sx_1", "sy", "freq"),
    )
    return jax.shard_map(
        on_device,
        mesh=finer,
        in_specs=(
            P("freq", SX_SY, None, None),
            P("freq", SX_SY, None, None),
            P(SX_SY, None),
            P("freq", SX, "sy", None, None),
            P("freq", SX, "sy", None, None),
            P("freq", SX, "sy", None, None),
        ),
        out_specs=(P("freq", SX, "sy", None, None), P()),
        check_vma=False,
    )
```

time: 237 us -> 192 us (0.81)
  blocking collectives: 151 us -> 13.1 us
  starting transfers between devices: 31.5 us -> 62.4 us
  waiting for transfers between devices: 15.2 us -> 36.4 us
  Pallas kernels: 0 us -> 18.3 us
  between operations: 2.63 us -> 12.9 us
  other arithmetic: 16.3 us -> 24.2 us
  local copies, waits for them, and re-layouts: 8.41 us -> 14 us
  matrix products: 11.3 us -> 8.54 us
    all_to_all x1, blocking collectives: 101 us -> 13.1 us  [summed(): return jnp.sum(lax.all_to_all(copies, axis, 0, 0, tiled=True), axis=0)]
    psum x4 -> x0, blocking collectives: 50 us -> none  [by_axis(): return functools.reduce(lax.psum, axes, x)]
    ppermute x8 -> x25, starting transfers between devices: 23.9 us -> 51.6 us  [the longest x16 23.5 us: turn(): return lax.ppermute(x, axis, [(i, (i + by) % SIDE) for i in range(SIDE)])]
    ppermute x8 -> x25, waiting for transfers between devices: 14.2 us -> 34.3 us  [the longest x4 14.7 us: neighbours(): lax.ppermute(x, axis, [(b, a) for a, b in up])]
    pallas_call x0 -> x2, Pallas kernels: none -> 18.3 us  [owner_products(): pl.pallas_call(functools.partial(products_kernel, plan), grid_spec=pltpu....]
    slice x1 -> x14, local copies, waits for them, and re-layouts: 0.03 us -> 11.6 us  [the longest x8 8.17 us: unpacked(): power = y[rows, 0].astype(jnp.float32)]
    select_n x3 -> x0, other arithmetic: 8.67 us -> none  [the longest x2 7.48 us: on_device(): basis_slots = jnp.take(update_basis, source_child, axis=1)]
    gather x2 -> x0, local copies, waits for them, and re-layouts: 8.35 us -> none  [the longest x1 7.6 us: on_device(): basis_slots = jnp.take(update_basis, source_child, axis=1)]
  transfers between devices with their start and end apart: 9 -> 26, of which waited for: 7 -> 13; matrix products, arithmetic and copies ran while one was open for 6% -> 13% of each run, Pallas kernels for 0% -> 7%
where the time goes in v1:
time: 192 us; the launch traced here: 190 us
  starting transfers between devices  62.4 us (32%)
  waiting for transfers between devices  36.4 us (19%)
  other arithmetic  24.2 us (13%)
  Pallas kernels  18.3 us (10%)
  local copies, waits for them, and re-layouts  14 us (7%)
  blocking collectives  13.1 us (7%)
  between operations  12.9 us (7%)
  matrix products  8.54 us (4%)
    ppermute x16, starting transfers between devices, turn(): return lax.ppermute(x, axis, [(i, (i + by) % SIDE) for i in range(SIDE)])  23.5 us
    pallas_call x2, Pallas kernels, owner_products(): pl.pallas_call(functools.partial(products_kernel, plan), grid_spec=pltpu....  18.3 us
    ppermute x4, starting transfers between devices, neighbours(): lax.ppermute(x, axis, up)  15 us
    ppermute x4, waiting for transfers between devices, neighbours(): lax.ppermute(x, axis, [(b, a) for a, b in up])  14.7 us
    ppermute x16, waiting for transfers between devices, turn(): return lax.ppermute(x, axis, [(i, (i + by) % SIDE) for i in range(SIDE)])  14.7 us
    all_to_all x1, blocking collectives, summed(): return jnp.sum(lax.all_to_all(copies, axis, 0, 0, tiled=True), axis=0)  13.1 us
    all_to_all x1, starting transfers between devices, summed(): return jnp.sum(lax.all_to_all(copies, axis, 0, 0, tiled=True), axis=0)  10.8 us
    dot_general x3, matrix products, apply_inverse(): jnp.einsum('fst,ftn->fsn', inverse_block, field.astype(jnp.bfloat16), pre...  8.54 us
  transfers between devices with their start and end apart: 26, of which 13 were waited for; matrix products, arithmetic and copies ran while one was open for 13% of the time, Pallas kernels for 7%

profile of v1, /device:TPU:1, one launch (start us, length us, event | category | flops | bytes accessed | tf_op | source)
XLA Modules:
  0.0 189.8 jit_solution(4349869707738318319)
XLA Ops:
  1.2 6.0 %shard_map.78 = (bf16[2,1024,128]{2,1,0:T(8,128)(2,1)}, bf16[2,1024,128]{2,1,0:T(8,128)(2,1)}, bf16[2,1024,128]{2,1,0:T(8,128)(2,1)}, bf16[2,1024,128]{2,1,0:T(8,128)(2,1)}) custom-call(s32[32]{0:T(128)} %bitcast.132, s32[2]{0:T(128)} %pad_add_fusion.place_ref, bf16[2,32,32,1024]{3,2,1,0:T(8,128)(2,1)} %basis_ref.3, bf16[2,32,32,128]{3,2,1,0:T(8,128)(2,1)} %coeff_ref.3), custom_call_target="tpu_custom_call" | custom-call | flops 1073741824 | bytes 6291456 | tf_op jit(solution)/shard_map/pallas_call | solution.py:94
  7.2 2.1 %collective-permute-start = (bf16[2,1024,128]{2,1,0:T(8,128)(2,1)}, bf16[2,1024,128]{2,1,0:T(8,128)(2,1)S(1)}, u32[]{:S(2)}, u32[]{:S(2)}) collective-permute-start(bf16[2,1024,128]{2,1,0:T(8,128)(2,1)} %get-tuple-element.62), channel_id=1, source_target_pairs={{0,64},{64,128},{128,192},{192,0},{1,65},{65,129},{129,193},{193,1... | collective-permute-start | bytes 1572872 | tf_op jit(solution)/shard_map/ppermute | solution.py:121
  9.4 1.4 collective-permute-start.2
  10.8 1.2 collective-permute-start.8
  12.0 1.5 collective-permute-start.10
  13.5 12.3 %shard_map.77 = (bf16[4,1024,128]{2,1,0:T(8,128)(2,1)}, bf16[4,1024,128]{2,1,0:T(8,128)(2,1)}, f32[4,1024,128]{2,1,0:T(8,128)}, bf16[4,1024,128]{2,1,0:T(8,128)(...) custom-call(s32[32]{0:T(128)} %bitcast.133, s32[2]{0:T(128)} %pad_add_fusion.place_ref, ...), custom_call_target="tpu_custom_call" | custom-call | flops 3221225472 | bytes 10485760 | tf_op jit(solution)/shard_map/pallas_call | solution.py:94
  25.8 2.1 %add_dynamic-update-slice_fusion.3 = bf16[4,1024,128]{2,1,0:T(8,128)(2,1)} fusion(bf16[4,1024,128]{2,1,0:T(8,128)(2,1)} %get-tuple-element.61, bf16[2,1024,128]{2,1,0:T(8,128)(2,1)S(1)} %collective-permute-done), kind=kLoop, calls=%fused_computation.51 | loop fusion | flops 1048576 | bytes 1572864 | tf_op jit(solution)/shard_map/scatter-add | solution.py:125
  28.0 2.0 %add_dynamic-update-slice_fusion.2 = bf16[4,1024,128]{2,1,0:T(8,128)(2,1)} fusion(bf16[4,1024,128]{2,1,0:T(8,128)(2,1)} %get-tuple-element.63, bf16[2,1024,128]{2,1,0:T(8,128)(2,1)S(1)} %collective-permute-done.2), kind=kLoop, calls=%fused_computation.50 | loop fusion | flops 1048576 | bytes 1572864 | tf_op jit(solution)/shard_map/scatter-add | solution.py:125
  30.0 2.7 %collective-permute-start.3 = (bf16[4,1024,128]{2,1,0:T(8,128)(2,1)}, bf16[4,1024,128]{2,1,0:T(8,128)(2,1)S(1)}, u32[]{:S(2)}, u32[]{:S(2)}) collective-permute-start(bf16[4,1024,128]{2,1,0:T(8,128)(2,1)} %add_dynamic-update-slice_fusion.2), channel_id=1, source_target_pairs={{0,192},{64,0},{128,64},{192,128},{1,193},{65,1},{129,65},{193,129... | collective-permute-start | bytes 3145736 | tf_op jit(solution)/shard_map/ppermute | solution.py:121
  32.6 2.0 %add_dynamic-update-slice_fusion.1 = bf16[4,1024,128]{2,1,0:T(8,128)(2,1)} fusion(bf16[4,1024,128]{2,1,0:T(8,128)(2,1)} %get-tuple-element.66, bf16[2,1024,128]{2,1,0:T(8,128)(2,1)S(1)} %collective-permute-done.8), kind=kLoop, calls=%fused_computation.43 | loop fusion | flops 1048576 | bytes 1572864 | tf_op jit(solution)/shard_map/scatter-add | solution.py:125
  34.7 2.0 %add_dynamic-update-slice_fusion = bf16[4,1024,128]{2,1,0:T(8,128)(2,1)} fusion(bf16[4,1024,128]{2,1,0:T(8,128)(2,1)} %get-tuple-element.68, bf16[2,1024,128]{2,1,0:T(8,128)(2,1)S(1)} %collective-permute-done.10), kind=kLoop, calls=%fused_computation.42 | loop fusion | flops 1048576 | bytes 1572864 | tf_op jit(solution)/shard_map/scatter-add | solution.py:125
  36.7 2.7 %collective-permute-start.11 = (bf16[4,1024,128]{2,1,0:T(8,128)(2,1)}, bf16[4,1024,128]{2,1,0:T(8,128)(2,1)}, u32[]{:S(2)}, u32[]{:S(2)}) collective-permute-start(bf16[4,1024,128]{2,1,0:T(8,128)(2,1)} %add_dynamic-update-slice_fusion), channel_id=1, source_target_pairs={{0,48},{16,0},{32,16},{48,32},{1,49},{17,1},{33,17},{49,33},{2,50}... | collective-permute-start | bytes 3145736 | tf_op jit(solution)/shard_map/ppermute | solution.py:121
  39.4 11.4 %collective-permute-done.1 = bf16[4,1024,128]{2,1,0:T(8,128)(2,1)S(1)} collective-permute-done((bf16[4,1024,128]{2,1,0:T(8,128)(2,1)}, bf16[4,1024,128]{2,1,0:T(8,128)(2,1)S(1)}, u32[]{:S(2)}, u32[]{:S(2)}) %collective-permute-start.1) | collective-permute-done | bytes 1048608 | tf_op jit(solution)/shard_map/ppermute | solution.py:121
  51.8 2.0 %abs_reduce_fusion.5 = (f32[]{:T(128)}, f32[1,1024,128]{2,1,0:T(8,128)}, f32[]{:T(128)}, f32[1,1024,128]{2,1,0:T(8,128)}, f32[]{:T(128)}, /*index=5*/f32[1,1024,128]{2,1,0:T(8,128)S(1)}) fusion(bf16[4,1024,128]{2,1,0:T(8,128)(2,1)S(1)} %collective-permute-done.3, bf16[4,1024,128]{2,1,0:T(8,128)(2,1)S(1)} %collective-permute-done.1, ...), kind=kLoop, calls=%fused_computation.47 | loop fusion | flops 2359293 | bytes 4718604 | tf_op jit(solution)/shard_map/reduce_max | solution.py:180
  57.9 3.3 %abs_reduce_fusion.2 = (f32[]{:T(128)}, f32[1,1024,128]{2,1,0:T(8,128)}, f32[]{:T(128)}, f32[1,1024,128]{2,1,0:T(8,128)}, f32[]{:T(128)}, /*index=5*/f32[1,1024,128]{2,1,0:T(8,128)S(1)}) fusion(bf16[4,1024,128]{2,1,0:T(8,128)(2,1)} %collective-permute-done.11, bf16[4,1024,128]{2,1,0:T(8,128)(2,1)} %collective-permute-done.9, f32[4,1024,128]{2,1,0:T(8,128)S(1)} %copy-done.2), kind=kLoop, calls=%fused_computation.39 | loop fusion | flops 2359293 | bytes 4718604 | tf_op jit(solution)/shard_map/reduce_max | solution.py:180
  64.0 2.4 %collective-permute-start.4 = (f16[528,128]{1,0:T(8,128)(2,1)}, f16[528,128]{1,0:T(8,128)(2,1)}, u32[]{:S(2)}, u32[]{:S(2)}) collective-permute-start(f16[528,128]{1,0:T(8,128)(2,1)} %concatenate.44), channel_id=1, source_target_pairs={{0,16},{16,32},{32,48},{48,0},{1,17},{17,33},{33,49},{49,1},{2,18}... | collective-permute-start | bytes 405512 | tf_op jit(solution)/shard_map/ppermute | solution.py:121
  69.8 2.7 %collective-permute-start.14 = (f16[528,128]{1,0:T(8,128)(2,1)S(1)}, f16[528,128]{1,0:T(8,128)(2,1)}, u32[]{:S(2)}, u32[]{:S(2)}) collective-permute-start(f16[528,128]{1,0:T(8,128)(2,1)S(1)} %concatenate.53), channel_id=1, source_target_pairs={{0,192},{64,0},{128,64},{192,128},{1,193},{65,1},{129,65},{193,129... | collective-permute-start | bytes 405512 | tf_op jit(solution)/shard_map/ppermute | solution.py:121
  73.5 1.2 slice.379
  75.4 1.2 slice.387
  77.3 1.2 slice.401
  83.1 2.3 %collective-permute-start.7 = (f16[1040,128]{1,0:T(8,128)(2,1)S(1)}, f16[1040,128]{1,0:T(8,128)(2,1)}, u32[]{:S(2)}, u32[]{:S(2)}) collective-permute-start(f16[1040,128]{1,0:T(8,128)(2,1)S(1)} %concatenate.49), channel_id=1, source_target_pairs={{0,48},{16,0},{32,16},{48,32},{1,49},{17,1},{33,17},{49,33},{2,50}... | collective-permute-start | bytes 798728 | tf_op jit(solution)/shard_map/ppermute | solution.py:121
  86.9 2.7 %collective-permute-start.15 = (f16[1040,128]{1,0:T(8,128)(2,1)S(1)}, f16[1040,128]{1,0:T(8,128)(2,1)S(1)}, u32[]{:S(2)}, u32[]{:S(2)}) collective-permute-start(f16[1040,128]{1,0:T(8,128)(2,1)S(1)} %concatenate.55), channel_id=1, source_target_pairs={{0,192},{64,0},{128,64},{192,128},{1,193},{65,1},{129,65},{193,129... | collective-permute-start | bytes 798728 | tf_op jit(solution)/shard_map/ppermute | solution.py:121
  89.7 1.2 slice.382
  91.6 1.2 slice.389
  96.1 1.5 fusion.31
  97.6 1.5 fusion.29
  99.1 1.3 fusion.53
  100.4 1.3 collective-permute-start.16
  101.7 1.3 collective-permute-start.17
  103.0 5.3 %collective-permute-start.18 = (bf16[2,1024,128]{2,1,0:T(8,128)(2,1)S(1)}, bf16[2,1024,128]{2,1,0:T(8,128)(2,1)S(1)}, u32[]{:S(2)}, u32[]{:S(2)}) collective-permute-start(bf16[2,1024,128]{2,1,0:T(8,128)(2,1)S(1)} %get-tuple-element.104), channel_id=1, source_target_pairs={{0,2},{2,4},{4,6},{6,8},{8,10},{10,12},{12,14},{1,3},{3,5},{5,7},{... | collective-permute-start | bytes 1572872 | tf_op jit(solution)/shard_map/ppermute | solution.py:147
  108.3 1.3 collective-permute-start.19
  109.7 1.9 %collective-permute-done.17 = bf16[2,1024,128]{2,1,0:T(8,128)(2,1)S(1)} collective-permute-done((bf16[2,1024,128]{2,1,0:T(8,128)(2,1)S(1)}, bf16[2,1024,128]{2,1,0:T(8,128)(2,1)S(1)}, u32[]{:S(2)}, u32[]{:S(2)}) %collective-permute-start.17) | collective-permute-done | bytes 524320 | tf_op jit(solution)/shard_map/ppermute | solution.py:147
  111.6 2.8 %collective-permute-done.18 = bf16[2,1024,128]{2,1,0:T(8,128)(2,1)S(1)} collective-permute-done((bf16[2,1024,128]{2,1,0:T(8,128)(2,1)S(1)}, bf16[2,1024,128]{2,1,0:T(8,128)(2,1)S(1)}, u32[]{:S(2)}, u32[]{:S(2)}) %collective-permute-start.18) | collective-permute-done | bytes 524320 | tf_op jit(solution)/shard_map/ppermute | solution.py:147
  114.4 4.3 %collective-permute-done.19 = bf16[2,1024,128]{2,1,0:T(8,128)(2,1)S(1)} collective-permute-done((bf16[2,1024,128]{2,1,0:T(8,128)(2,1)S(1)}, bf16[2,1024,128]{2,1,0:T(8,128)(2,1)S(1)}, u32[]{:S(2)}, u32[]{:S(2)}) %collective-permute-start.19) | collective-permute-done | bytes 524320 | tf_op jit(solution)/shard_map/ppermute | solution.py:147
  118.7 2.8 %fusion.54 = (bf16[2,1024,128]{2,1,0:T(8,128)(2,1)}, f32[2,1024,128]{2,1,0:T(8,128)S(1)}) fusion(f32[2,1024,128]{2,1,0:T(8,128)S(1)} %get-tuple-element.105, bf16[2,1024,128]{2,1,0:T(8,128)(2,1)S(1)} %collective-permute-done.19, bf16[2,1024,128]{2,1,0:T(8,128)(2,1)S(1)} %collective-permute-done.18, bf16[2,1024,128]{2,1,0:T(8,128)(2,1)S(1)} %collective-permute-done.17, ...), kind=kOutput, calls=%fused_computation.87 | convolution fusion | flops 541851648 | bytes 10518528 | tf_op jit(solution)/shard_map/fst,ftn->fsn/dot_general | solution.py:196
  121.5 3.7 %collective-permute-start.20 = (bf16[2,1024,128]{2,1,0:T(8,128)(2,1)}, bf16[2,1024,128]{2,1,0:T(8,128)(2,1)S(1)}, u32[]{:S(2)}, u32[]{:S(2)}) collective-permute-start(bf16[2,1024,128]{2,1,0:T(8,128)(2,1)} %get-tuple-element.106), channel_id=1, source_target_pairs={{0,16},{16,32},{32,48},{48,64},{64,80},{80,96},{96,112},{112,128},... | collective-permute-start | bytes 1572872 | tf_op jit(solution)/shard_map/ppermute | solution.py:147
  125.2 1.3 collective-permute-start.21
  126.5 4.6 %collective-permute-start.22 = (bf16[2,1024,128]{2,1,0:T(8,128)(2,1)}, bf16[2,1024,128]{2,1,0:T(8,128)(2,1)}, u32[]{:S(2)}, u32[]{:S(2)}) collective-permute-start(bf16[2,1024,128]{2,1,0:T(8,128)(2,1)} %get-tuple-element.106), channel_id=1, source_target_pairs={{0,2},{2,4},{4,6},{6,8},{8,10},{10,12},{12,14},{1,3},{3,5},{5,7},{... | collective-permute-start | bytes 1572872 | tf_op jit(solution)/shard_map/ppermute | solution.py:147
  131.2 1.3 collective-permute-start.23
  132.5 3.0 %collective-permute-done.21 = bf16[2,1024,128]{2,1,0:T(8,128)(2,1)} collective-permute-done((bf16[2,1024,128]{2,1,0:T(8,128)(2,1)}, bf16[2,1024,128]{2,1,0:T(8,128)(2,1)}, u32[]{:S(2)}, u32[]{:S(2)}) %collective-permute-start.21) | collective-permute-done | bytes 524320 | tf_op jit(solution)/shard_map/ppermute | solution.py:147
  135.5 1.3 collective-permute-done.22
  136.8 5.5 %collective-permute-done.23 = bf16[2,1024,128]{2,1,0:T(8,128)(2,1)} collective-permute-done((bf16[2,1024,128]{2,1,0:T(8,128)(2,1)}, bf16[2,1024,128]{2,1,0:T(8,128)(2,1)}, u32[]{:S(2)}, u32[]{:S(2)}) %collective-permute-start.23) | collective-permute-done | bytes 524320 | tf_op jit(solution)/shard_map/ppermute | solution.py:147
  142.3 3.4 %multiply_reduce_fusion = (f32[2]{0:T(128)S(1)}, bf16[2,1024,128]{2,1,0:T(8,128)(2,1)S(1)}) fusion(bf16[2,1024,128]{2,1,0:T(8,128)(2,1)} %collective-permute-done.23, f32[2,1024]{1,0:T(2,128)S(1)} %get-tuple-element.112, bf16[2,1024,128]{2,1,0:T(8,128)(2,1)} %collective-permute-done.22, f32[2,1024]{1,0:T(2,128)S(1)} %get-tuple-element.113, ...), kind=kLoop, calls=%fused_computation.13 | loop fusion | flops 4980734 | bytes 5275656 | tf_op jit(solution)/shard_map/reduce_sum | solution.py:214
  147.0 7.9 %collective-permute-start.24 = (f32[8,128]{1,0:T(8,128)S(1)}, f32[8,128]{1,0:T(8,128)S(1)}, u32[]{:S(2)}, u32[]{:S(2)}) collective-permute-start(f32[8,128]{1,0:T(8,128)S(1)} %broadcast_in_dim.9), channel_id=1, source_target_pairs={{0,1},{1,0},{2,3},{3,2},{4,5},{5,4},{6,7},{7,6},{8,9},{9,8},{10,11... | collective-permute-start | bytes 12296 | tf_op jit(solution)/shard_map/ppermute | solution.py:216
  156.4 13.1 %all_to_all.10 = f32[8,8,128]{2,1,0:T(8,128)S(1)} all-to-all(f32[8,8,128]{2,1,0:T(8,128)S(1)} %broadcast_in_dim.10), channel_id=1, replica_groups=mesh['sx_0'=4,'sx_1'=4,'sy'=8,'freq'=2] {'sy'}, dimensions={0} | all-to-all | bytes 65536 | tf_op jit(solution)/shard_map/all_to_all | solution.py:142
  170.1 10.8 %all-to-all-start.1 = ((f32[16,8,128]{2,1,0:T(8,128)}), f32[16,8,128]{2,1,0:T(8,128)S(1)}, u32[]{:S(2)}, u32[]{:S(2)}) async-start(f32[16,8,128]{2,1,0:T(8,128)} %broadcast_in_dim.11), calls=%async_computation.1 | async-start | bytes 131072 | tf_op jit(solution)/shard_map/all_to_all | solution.py:142
  180.9 4.4 %fusion.12 = f32[2,1,1,1024,128]{4,3,2,1,0:T(8,128)} fusion(f32[2,1024,128]{2,1,0:T(8,128)S(1)} %get-tuple-element.107, bf16[2,1,1,1024,1024]{4,3,2,1,0:T(8,128)(2,1)} %param.19, bf16[2,1024,128]{2,1,0:T(8,128)(2,1)S(1)} %get-tuple-element.75), kind=kOutput, calls=%fused_computation.8 | convolution fusion | flops 537133056 | bytes 6815744 | tf_op jit(solution)/shard_map/fst,ftn->fsn/dot_general | solution.py:196
  185.3 2.1 %all-to-all-done.1 = f32[16,8,128]{2,1,0:T(8,128)S(1)} async-done(((f32[16,8,128]{2,1,0:T(8,128)}), f32[16,8,128]{2,1,0:T(8,128)S(1)}, u32[]{:S(2)}, u32[]{:S(2)}) %all-to-all-start.1) | async-done | bytes 65568 | tf_op jit(solution)/shard_map/all_to_all | solution.py:142
  (85 shorter events, 18.3 us)
Async XLA Ops:
  7.2 18.6 %collective-permute-start = (bf16[2,1024,128]{2,1,0:T(8,128)(2,1)}, bf16[2,1024,128]{2,1,0:T(8,128)(2,1)S(1)}, u32[]{:S(2)}, u32[]{:S(2)}) collective-permute-start(bf16[2,1024,128]{2,1,0:T(8,128)(2,1)} %get-tuple-element.62), channel_id=1, source_target_pairs={{0,64},{64,128},{128,192},{192,0},{1,65},{65,129},{129,193},{193,1... | collective-permute-start | bytes 1572872 | tf_op jit(solution)/shard_map/ppermute | solution.py:121
  9.4 18.6 %collective-permute-start.2 = (bf16[2,1024,128]{2,1,0:T(8,128)(2,1)}, bf16[2,1024,128]{2,1,0:T(8,128)(2,1)S(1)}, u32[]{:S(2)}, u32[]{:S(2)}) collective-permute-start(bf16[2,1024,128]{2,1,0:T(8,128)(2,1)} %get-tuple-element.64), channel_id=1, source_target_pairs={{0,192},{64,0},{128,64},{192,128},{1,193},{65,1},{129,65},{193,129... | collective-permute-start | bytes 1572872 | tf_op jit(solution)/shard_map/ppermute | solution.py:121
  10.8 21.8 %collective-permute-start.8 = (bf16[2,1024,128]{2,1,0:T(8,128)(2,1)}, bf16[2,1024,128]{2,1,0:T(8,128)(2,1)S(1)}, u32[]{:S(2)}, u32[]{:S(2)}) collective-permute-start(bf16[2,1024,128]{2,1,0:T(8,128)(2,1)} %get-tuple-element.67), channel_id=1, source_target_pairs={{0,16},{16,32},{32,48},{48,0},{1,17},{17,33},{33,49},{49,1},{2,18}... | collective-permute-start | bytes 1572872 | tf_op jit(solution)/shard_map/ppermute | solution.py:121
  12.0 22.7 %collective-permute-start.10 = (bf16[2,1024,128]{2,1,0:T(8,128)(2,1)}, bf16[2,1024,128]{2,1,0:T(8,128)(2,1)S(1)}, u32[]{:S(2)}, u32[]{:S(2)}) collective-permute-start(bf16[2,1024,128]{2,1,0:T(8,128)(2,1)} %get-tuple-element.69), channel_id=1, source_target_pairs={{0,48},{16,0},{32,16},{48,32},{1,49},{17,1},{33,17},{49,33},{2,50}... | collective-permute-start | bytes 1572872 | tf_op jit(solution)/shard_map/ppermute | solution.py:121
  25.8 25.9 %copy-start.3 = (f32[4,1024,128]{2,1,0:T(8,128)S(1)}, f32[4,1024,128]{2,1,0:T(8,128)}, u32[]{:S(2)}) copy-start(f32[4,1024,128]{2,1,0:T(8,128)} %get-tuple-element.60) | copy-start | bytes 6291460
  28.0 22.8 %collective-permute-start.1 = (bf16[4,1024,128]{2,1,0:T(8,128)(2,1)}, bf16[4,1024,128]{2,1,0:T(8,128)(2,1)S(1)}, u32[]{:S(2)}, u32[]{:S(2)}) collective-permute-start(bf16[4,1024,128]{2,1,0:T(8,128)(2,1)} %add_dynamic-update-slice_fusion.3), channel_id=1, source_target_pairs={{0,64},{64,128},{128,192},{192,0},{1,65},{65,129},{129,193},{193,1... | collective-permute-start | bytes 3145736 | tf_op jit(solution)/shard_map/ppermute | solution.py:121
  30.0 28.0 %copy-start.2 = (f32[4,1024,128]{2,1,0:T(8,128)S(1)}, f32[4,1024,128]{2,1,0:T(8,128)}, u32[]{:S(2)}) copy-start(f32[4,1024,128]{2,1,0:T(8,128)} %get-tuple-element.65) | copy-start | bytes 6291460
  30.0 21.8 %collective-permute-start.3 = (bf16[4,1024,128]{2,1,0:T(8,128)(2,1)}, bf16[4,1024,128]{2,1,0:T(8,128)(2,1)S(1)}, u32[]{:S(2)}, u32[]{:S(2)}) collective-permute-start(bf16[4,1024,128]{2,1,0:T(8,128)(2,1)} %add_dynamic-update-slice_fusion.2), channel_id=1, source_target_pairs={{0,192},{64,0},{128,64},{192,128},{1,193},{65,1},{129,65},{193,129... | collective-permute-start | bytes 3145736 | tf_op jit(solution)/shard_map/ppermute | solution.py:121
  34.7 22.2 %collective-permute-start.9 = (bf16[4,1024,128]{2,1,0:T(8,128)(2,1)}, bf16[4,1024,128]{2,1,0:T(8,128)(2,1)}, u32[]{:S(2)}, u32[]{:S(2)}) collective-permute-start(bf16[4,1024,128]{2,1,0:T(8,128)(2,1)} %add_dynamic-update-slice_fusion.1), channel_id=1, source_target_pairs={{0,16},{16,32},{32,48},{48,0},{1,17},{17,33},{33,49},{49,1},{2,18}... | collective-permute-start | bytes 3145736 | tf_op jit(solution)/shard_map/ppermute | solution.py:121
  36.7 21.2 %collective-permute-start.11 = (bf16[4,1024,128]{2,1,0:T(8,128)(2,1)}, bf16[4,1024,128]{2,1,0:T(8,128)(2,1)}, u32[]{:S(2)}, u32[]{:S(2)}) collective-permute-start(bf16[4,1024,128]{2,1,0:T(8,128)(2,1)} %add_dynamic-update-slice_fusion), channel_id=1, source_target_pairs={{0,48},{16,0},{32,16},{48,32},{1,49},{17,1},{33,17},{49,33},{2,50}... | collective-permute-start | bytes 3145736 | tf_op jit(solution)/shard_map/ppermute | solution.py:121
  50.8 3.0 %copy-start.8 = (bf16[4,1024,128]{2,1,0:T(8,128)(2,1)}, bf16[4,1024,128]{2,1,0:T(8,128)(2,1)S(1)}, u32[]{:S(2)}) copy-start(bf16[4,1024,128]{2,1,0:T(8,128)(2,1)S(1)} %collective-permute-done.1) | copy-start | bytes 3145732
  51.7 2.0 %copy-start.9 = (bf16[4,1024,128]{2,1,0:T(8,128)(2,1)}, bf16[4,1024,128]{2,1,0:T(8,128)(2,1)S(1)}, u32[]{:S(2)}) copy-start(bf16[4,1024,128]{2,1,0:T(8,128)(2,1)S(1)} %collective-permute-done.3) | copy-start | bytes 3145732
  61.2 12.3 %copy-start.5 = (f32[1,1024,128]{2,1,0:T(8,128)S(1)}, f32[1,1024,128]{2,1,0:T(8,128)}, u32[]{:S(2)}) copy-start(f32[1,1024,128]{2,1,0:T(8,128)} %get-tuple-element.93) | copy-start | bytes 1572868
  61.2 19.9 %copy-start.6 = (f32[1,1024,128]{2,1,0:T(8,128)S(1)}, f32[1,1024,128]{2,1,0:T(8,128)}, u32[]{:S(2)}) copy-start(f32[1,1024,128]{2,1,0:T(8,128)} %get-tuple-element.81) | copy-start | bytes 1572868
  61.2 19.9 %copy-start.7 = (f32[1,1024,128]{2,1,0:T(8,128)S(1)}, f32[1,1024,128]{2,1,0:T(8,128)}, u32[]{:S(2)}) copy-start(f32[1,1024,128]{2,1,0:T(8,128)} %get-tuple-element.89) | copy-start | bytes 1572868
  63.3 22.2 %copy-start.4 = (f32[1,1024,128]{2,1,0:T(8,128)S(1)}, f32[1,1024,128]{2,1,0:T(8,128)}, u32[]{:S(2)}) copy-start(f32[1,1024,128]{2,1,0:T(8,128)} %get-tuple-element.87) | copy-start | bytes 1572868
  64.0 9.5 %collective-permute-start.4 = (f16[528,128]{1,0:T(8,128)(2,1)}, f16[528,128]{1,0:T(8,128)(2,1)}, u32[]{:S(2)}, u32[]{:S(2)}) collective-permute-start(f16[528,128]{1,0:T(8,128)(2,1)} %concatenate.44), channel_id=1, source_target_pairs={{0,16},{16,32},{32,48},{48,0},{1,17},{17,33},{33,49},{49,1},{2,18}... | collective-permute-start | bytes 405512 | tf_op jit(solution)/shard_map/ppermute | solution.py:121
  66.5 8.9 %collective-permute-start.6 = (f16[528,128]{1,0:T(8,128)(2,1)S(1)}, f16[528,128]{1,0:T(8,128)(2,1)}, u32[]{:S(2)}, u32[]{:S(2)}) collective-permute-start(f16[528,128]{1,0:T(8,128)(2,1)S(1)} %concatenate.47), channel_id=1, source_target_pairs={{0,48},{16,0},{32,16},{48,32},{1,49},{17,1},{33,17},{49,33},{2,50}... | collective-permute-start | bytes 405512 | tf_op jit(solution)/shard_map/ppermute | solution.py:121
  69.7 7.6 %collective-permute-start.12 = (f16[528,128]{1,0:T(8,128)(2,1)S(1)}, f16[528,128]{1,0:T(8,128)(2,1)}, u32[]{:S(2)}, u32[]{:S(2)}) collective-permute-start(f16[528,128]{1,0:T(8,128)(2,1)S(1)} %concatenate.50), channel_id=1, source_target_pairs={{0,64},{64,128},{128,192},{192,0},{1,65},{65,129},{129,193},{193,1... | collective-permute-start | bytes 405512 | tf_op jit(solution)/shard_map/ppermute | solution.py:121
  69.8 9.3 %collective-permute-start.14 = (f16[528,128]{1,0:T(8,128)(2,1)S(1)}, f16[528,128]{1,0:T(8,128)(2,1)}, u32[]{:S(2)}, u32[]{:S(2)}) collective-permute-start(f16[528,128]{1,0:T(8,128)(2,1)S(1)} %concatenate.53), channel_id=1, source_target_pairs={{0,192},{64,0},{128,64},{192,128},{1,193},{65,1},{129,65},{193,129... | collective-permute-start | bytes 405512 | tf_op jit(solution)/shard_map/ppermute | solution.py:121
  82.3 7.4 %collective-permute-start.5 = (f16[1040,128]{1,0:T(8,128)(2,1)S(1)}, f16[1040,128]{1,0:T(8,128)(2,1)}, u32[]{:S(2)}, u32[]{:S(2)}) collective-permute-start(f16[1040,128]{1,0:T(8,128)(2,1)S(1)} %concatenate.46), channel_id=1, source_target_pairs={{0,16},{16,32},{32,48},{48,0},{1,17},{17,33},{33,49},{49,1},{2,18}... | collective-permute-start | bytes 798728 | tf_op jit(solution)/shard_map/ppermute | solution.py:121
  83.0 16.0 %copy-start.1 = (bf16[2,1,1,1024,128]{4,3,2,1,0:T(8,128)(2,1)S(1)}, bf16[2,1,1,1024,128]{4,3,2,1,0:T(8,128)(2,1)}, u32[]{:S(2)}) copy-start(bf16[2,1,1,1024,128]{4,3,2,1,0:T(8,128)(2,1)} %param.17) | copy-start | bytes 1572868
  83.1 8.5 %collective-permute-start.7 = (f16[1040,128]{1,0:T(8,128)(2,1)S(1)}, f16[1040,128]{1,0:T(8,128)(2,1)}, u32[]{:S(2)}, u32[]{:S(2)}) collective-permute-start(f16[1040,128]{1,0:T(8,128)(2,1)S(1)} %concatenate.49), channel_id=1, source_target_pairs={{0,48},{16,0},{32,16},{48,32},{1,49},{17,1},{33,17},{49,33},{2,50}... | collective-permute-start | bytes 798728 | tf_op jit(solution)/shard_map/ppermute | solution.py:121
  86.6 7.0 %collective-permute-start.13 = (f16[1040,128]{1,0:T(8,128)(2,1)S(1)}, f16[1040,128]{1,0:T(8,128)(2,1)S(1)}, u32[]{:S(2)}, u32[]{:S(2)}) collective-permute-start(f16[1040,128]{1,0:T(8,128)(2,1)S(1)} %concatenate.52), channel_id=1, source_target_pairs={{0,64},{64,128},{128,192},{192,0},{1,65},{65,129},{129,193},{193,1... | collective-permute-start | bytes 798728 | tf_op jit(solution)/shard_map/ppermute | solution.py:121
  86.8 12.2 %copy-start = (bf16[2,1,1,1024,1024]{4,3,2,1,0:T(8,128)(2,1)S(1)}, bf16[2,1,1,1024,1024]{4,3,2,1,0:T(8,128)(2,1)}, u32[]{:S(2)}) copy-start(bf16[2,1,1,1024,1024]{4,3,2,1,0:T(8,128)(2,1)} %param.19) | copy-start | bytes 12582916
  86.9 7.9 %collective-permute-start.15 = (f16[1040,128]{1,0:T(8,128)(2,1)S(1)}, f16[1040,128]{1,0:T(8,128)(2,1)S(1)}, u32[]{:S(2)}, u32[]{:S(2)}) collective-permute-start(f16[1040,128]{1,0:T(8,128)(2,1)S(1)} %concatenate.55), channel_id=1, source_target_pairs={{0,192},{64,0},{128,64},{192,128},{1,193},{65,1},{129,65},{193,129... | collective-permute-start | bytes 798728 | tf_op jit(solution)/shard_map/ppermute | solution.py:121
  93.6 4.0 %copy-start.11 = (f16[1040,128]{1,0:T(8,128)(2,1)}, f16[1040,128]{1,0:T(8,128)(2,1)S(1)}, u32[]{:S(2)}) copy-start(f16[1040,128]{1,0:T(8,128)(2,1)S(1)} %collective-permute-done.13) | copy-start | bytes 798724
  99.1 10.5 %copy-start.12 = (f32[2,1,1,4,1024]{4,3,2,1,0:T(4,128)S(1)}, f32[2,1,1,4,1024]{4,3,2,1,0:T(4,128)}, u32[]{:S(2)}) copy-start(f32[2,1,1,4,1024]{4,3,2,1,0:T(4,128)} %param.18) | copy-start | bytes 98308
  100.4 9.3 %collective-permute-start.16 = (bf16[2,1024,128]{2,1,0:T(8,128)(2,1)S(1)}, bf16[2,1024,128]{2,1,0:T(8,128)(2,1)S(1)}, u32[]{:S(2)}, u32[]{:S(2)}) collective-permute-start(bf16[2,1024,128]{2,1,0:T(8,128)(2,1)S(1)} %get-tuple-element.104), channel_id=1, source_target_pairs={{0,16},{16,32},{32,48},{48,64},{64,80},{80,96},{96,112},{112,128},... | collective-permute-start | bytes 1572872 | tf_op jit(solution)/shard_map/ppermute | solution.py:147
  101.7 9.9 %collective-permute-start.17 = (bf16[2,1024,128]{2,1,0:T(8,128)(2,1)S(1)}, bf16[2,1024,128]{2,1,0:T(8,128)(2,1)S(1)}, u32[]{:S(2)}, u32[]{:S(2)}) collective-permute-start(bf16[2,1024,128]{2,1,0:T(8,128)(2,1)S(1)} %get-tuple-element.104), channel_id=1, source_target_pairs={{16,0},{32,16},{48,32},{64,48},{80,64},{96,80},{112,96},{128,112},... | collective-permute-start | bytes 1572872 | tf_op jit(solution)/shard_map/ppermute | solution.py:147
  103.0 11.4 %collective-permute-start.18 = (bf16[2,1024,128]{2,1,0:T(8,128)(2,1)S(1)}, bf16[2,1024,128]{2,1,0:T(8,128)(2,1)S(1)}, u32[]{:S(2)}, u32[]{:S(2)}) collective-permute-start(bf16[2,1024,128]{2,1,0:T(8,128)(2,1)S(1)} %get-tuple-element.104), channel_id=1, source_target_pairs={{0,2},{2,4},{4,6},{6,8},{8,10},{10,12},{12,14},{1,3},{3,5},{5,7},{... | collective-permute-start | bytes 1572872 | tf_op jit(solution)/shard_map/ppermute | solution.py:147
  108.3 10.4 %collective-permute-start.19 = (bf16[2,1024,128]{2,1,0:T(8,128)(2,1)S(1)}, bf16[2,1024,128]{2,1,0:T(8,128)(2,1)S(1)}, u32[]{:S(2)}, u32[]{:S(2)}) collective-permute-start(bf16[2,1024,128]{2,1,0:T(8,128)(2,1)S(1)} %get-tuple-element.104), channel_id=1, source_target_pairs={{2,0},{4,2},{6,4},{8,6},{10,8},{12,10},{14,12},{3,1},{5,3},{7,5},{... | collective-permute-start | bytes 1572872 | tf_op jit(solution)/shard_map/ppermute | solution.py:147
  121.5 11.0 %collective-permute-start.20 = (bf16[2,1024,128]{2,1,0:T(8,128)(2,1)}, bf16[2,1024,128]{2,1,0:T(8,128)(2,1)S(1)}, u32[]{:S(2)}, u32[]{:S(2)}) collective-permute-start(bf16[2,1024,128]{2,1,0:T(8,128)(2,1)} %get-tuple-element.106), channel_id=1, source_target_pairs={{0,16},{16,32},{32,48},{48,64},{64,80},{80,96},{96,112},{112,128},... | collective-permute-start | bytes 1572872 | tf_op jit(solution)/shard_map/ppermute | solution.py:147
  125.2 10.2 %collective-permute-start.21 = (bf16[2,1024,128]{2,1,0:T(8,128)(2,1)}, bf16[2,1024,128]{2,1,0:T(8,128)(2,1)}, u32[]{:S(2)}, u32[]{:S(2)}) collective-permute-start(bf16[2,1024,128]{2,1,0:T(8,128)(2,1)} %get-tuple-element.106), channel_id=1, source_target_pairs={{16,0},{32,16},{48,32},{64,48},{80,64},{96,80},{112,96},{128,112},... | collective-permute-start | bytes 1572872 | tf_op jit(solution)/shard_map/ppermute | solution.py:147
  126.5 10.2 %collective-permute-start.22 = (bf16[2,1024,128]{2,1,0:T(8,128)(2,1)}, bf16[2,1024,128]{2,1,0:T(8,128)(2,1)}, u32[]{:S(2)}, u32[]{:S(2)}) collective-permute-start(bf16[2,1024,128]{2,1,0:T(8,128)(2,1)} %get-tuple-element.106), channel_id=1, source_target_pairs={{0,2},{2,4},{4,6},{6,8},{8,10},{10,12},{12,14},{1,3},{3,5},{5,7},{... | collective-permute-start | bytes 1572872 | tf_op jit(solution)/shard_map/ppermute | solution.py:147
  131.2 11.1 %collective-permute-start.23 = (bf16[2,1024,128]{2,1,0:T(8,128)(2,1)}, bf16[2,1024,128]{2,1,0:T(8,128)(2,1)}, u32[]{:S(2)}, u32[]{:S(2)}) collective-permute-start(bf16[2,1024,128]{2,1,0:T(8,128)(2,1)} %get-tuple-element.106), channel_id=1, source_target_pairs={{2,0},{4,2},{6,4},{8,6},{10,8},{12,10},{14,12},{3,1},{5,3},{7,5},{... | collective-permute-start | bytes 1572872 | tf_op jit(solution)/shard_map/ppermute | solution.py:147
  132.5 9.8 %copy-start.10 = (bf16[2,1024,128]{2,1,0:T(8,128)(2,1)}, bf16[2,1024,128]{2,1,0:T(8,128)(2,1)S(1)}, u32[]{:S(2)}) copy-start(bf16[2,1024,128]{2,1,0:T(8,128)(2,1)S(1)} %collective-permute-done.20) | copy-start | bytes 1572868
  147.0 8.8 %collective-permute-start.24 = (f32[8,128]{1,0:T(8,128)S(1)}, f32[8,128]{1,0:T(8,128)S(1)}, u32[]{:S(2)}, u32[]{:S(2)}) collective-permute-start(f32[8,128]{1,0:T(8,128)S(1)} %broadcast_in_dim.9), channel_id=1, source_target_pairs={{0,1},{1,0},{2,3},{3,2},{4,5},{5,4},{6,7},{7,6},{8,9},{9,8},{10,11... | collective-permute-start | bytes 12296 | tf_op jit(solution)/shard_map/ppermute | solution.py:216
  170.1 17.3 %all-to-all-start.1 = ((f32[16,8,128]{2,1,0:T(8,128)}), f32[16,8,128]{2,1,0:T(8,128)S(1)}, u32[]{:S(2)}, u32[]{:S(2)}) async-start(f32[16,8,128]{2,1,0:T(8,128)} %broadcast_in_dim.11), calls=%async_computation.1 | async-start | bytes 131072 | tf_op jit(solution)/shard_map/all_to_all | solution.py:142

commit v2 on v1

v2 whole, which is shorter than its diff:
```python
import functools

import jax
import jax.numpy as jnp
from jax import lax
from jax.experimental import pallas as pl
from jax.experimental.pallas import tpu as pltpu
from jax.sharding import Mesh
from jax.sharding import PartitionSpec as P


SWEEPS = 2
SIDE = 4
CAP = 4
TILE = 256
SX = ("sx_0", "sx_1")
SX_SY = ("sx_0", "sx_1", "sy")
LOW, HIGH = (0, 1), (3, 2)


def cost(flops, bytes_accessed):
    return pl.CostEstimate(flops=flops, bytes_accessed=bytes_accessed, transcendentals=0)


def room(mebibytes):
    return pltpu.CompilerParams(vmem_limit_bytes=mebibytes << 20)


def products_kernel(plan, owner_ref, place_ref, basis_ref, coeff_ref, *rest):
    outs = rest[: len(plan)]
    slots, used, stacked, weights = rest[-4:]
    children = owner_ref.shape[0]
    rank = basis_ref.shape[2]
    rhs_count = coeff_ref.shape[3]
    step = pl.program_id(0)

    @pl.when(step == 0)
    def _():
        for o in range(SIDE * SIDE):
            used[o] = 0
        for s in range(SIDE * SIDE * CAP):
            slots[s] = children

        def put(c, carry):
            o = owner_ref[c]
            k = used[o]
            slots[o * CAP + k] = c
            used[o] = k + 1
            return carry

        lax.fori_loop(0, children, put, 0)
        weights[...] = jnp.zeros_like(weights)

    first = 0
    for out, (f, ahead, pairs) in zip(outs, plan, strict=True):
        for n, pair in enumerate(pairs):

            @pl.when(step == first + n)
            def _(out=out, f=f, ahead=ahead, pair=pair):
                for b, beside in enumerate(pair):
                    offsets = (ahead, beside) if f == 0 else (beside, ahead)
                    row = lax.rem(place_ref[0] + offsets[0], SIDE)
                    column = lax.rem(place_ref[1] + offsets[1], SIDE)
                    o = row * SIDE + column
                    for k in range(CAP):
                        c = slots[o * CAP + k]
                        filled = c < children
                        c = jnp.where(filled, c, 0)
                        at = (b * CAP + k) * rank
                        stacked[at : at + rank, :] = basis_ref[f, c]
                        coeff = coeff_ref[f, c]
                        weights[at : at + rank, b * rhs_count : (b + 1) * rhs_count] = jnp.where(
                            filled, coeff, jnp.zeros_like(coeff)
                        )
                turned = weights[...].T
                for s in range(0, stacked.shape[1], TILE):
                    product = jnp.dot(
                        turned, stacked[:, s : s + TILE], preferred_element_type=jnp.float32
                    )
                    for b in range(2):
                        piece = product[b * rhs_count : (b + 1) * rhs_count]
                        out[b, :, s : s + TILE] = piece.astype(out.dtype)

        first += len(pairs)


def owner_products(plan, dtypes, owners, place, basis, coeff, after=(), skipped=None):
    f_local, children, rank, sep_size = basis.shape
    rhs_count = coeff.shape[3]
    steps = sum(len(pairs) for _, _, pairs in plan)
    out_specs, out_shape, first, written = [], [], 0, 0
    for at, ((_, _, pairs), dtype) in enumerate(zip(plan, dtypes, strict=True)):
        n, base = len(pairs), skipped[at] if skipped else 0
        out_specs.append(
            pl.BlockSpec(
                (2, rhs_count, sep_size),
                lambda i, *_, first=first, n=n, base=base: (jnp.clip(i - first, 0, n - 1) + base, 0, 0),
            )
        )
        out_shape.append(jax.ShapeDtypeStruct((2 * (n + base), rhs_count, sep_size), dtype))
        written += 2 * n * rhs_count * sep_size * jnp.dtype(dtype).itemsize
        first += n

    def body(owner_ref, place_ref, basis_ref, coeff_ref, *rest):
        products_kernel(plan, owner_ref, place_ref, basis_ref, coeff_ref, *rest[len(after) :])

    return pl.pallas_call(
        body,
        grid_spec=pltpu.PrefetchScalarGridSpec(
            num_scalar_prefetch=2,
            grid=(steps,),
            in_specs=[
                pl.BlockSpec((f_local, children, rank, sep_size), lambda i, *_: (0, 0, 0, 0)),
                pl.BlockSpec((f_local, children, rank, rhs_count), lambda i, *_: (0, 0, 0, 0)),
            ]
            + [pl.BlockSpec(memory_space=pl.ANY) for _ in after],
            out_specs=out_specs,
            scratch_shapes=[
                pltpu.SMEM((SIDE * SIDE * CAP,), jnp.int32),
                pltpu.SMEM((SIDE * SIDE,), jnp.int32),
                pltpu.VMEM((2 * CAP * rank, sep_size), jnp.bfloat16),
                pltpu.VMEM((2 * CAP * rank, 2 * rhs_count), jnp.bfloat16),
            ],
        ),
        out_shape=out_shape,
        compiler_params=room(32),
        cost_estimate=cost(
            2 * steps * 4 * CAP * rank * sep_size * rhs_count * 2, basis.size * 2 + written
        ),
    )(owners, place, basis, coeff, *after)


def join(mine, got, whole):
    def body(mine_ref, got_ref, whole_ref, out_ref):
        out_ref[...] = (mine_ref[...] + got_ref[...].astype(jnp.float32)).astype(out_ref.dtype)

    n = mine.shape[0]
    block = (1, *mine.shape[1:])
    spec = pl.BlockSpec(block, lambda i: (i, 0, 0))
    return pl.pallas_call(
        body,
        grid=(n,),
        in_specs=[spec, spec, pl.BlockSpec(memory_space=pl.ANY)],
        out_specs=spec,
        out_shape=jax.ShapeDtypeStruct(whole.shape, whole.dtype),
        input_output_aliases={2: 0},
        compiler_params=room(8),
        cost_estimate=cost(mine.size * 2, mine.size * 8),
    )(mine, got, whole)


def row_totals(own, low, high):
    _, rhs_count, sep_size = own.shape
    half = rhs_count // 2

    def body(own_ref, low_ref, high_ref, here, following, preceding, one_way, other_way):
        def total(at):
            crossed = (at + 2) % SIDE
            return own_ref[at] + low_ref[at].astype(jnp.float32) + high_ref[crossed].astype(jnp.float32)

        here[...] = total(0)
        following[...] = total(1)
        preceding[...] = total(2)
        opposite = total(3).astype(jnp.bfloat16)
        one_way[...] = opposite[:half]
        other_way[...] = opposite[half:]

    whole = jax.ShapeDtypeStruct((rhs_count, sep_size), jnp.float32)
    part = jax.ShapeDtypeStruct((half, sep_size), jnp.bfloat16)
    stack = pl.BlockSpec((SIDE, rhs_count, TILE), lambda i: (0, 0, i))
    return pl.pallas_call(
        body,
        grid=(sep_size // TILE,),
        in_specs=[stack] * 3,
        out_specs=[pl.BlockSpec((rhs_count, TILE), lambda i: (0, i))] * 3
        + [pl.BlockSpec((half, TILE), lambda i: (0, i))] * 2,
        out_shape=[whole] * 3 + [part] * 2,
        compiler_params=room(12),
        cost_estimate=cost(own.size * 2, own.size * 12),
    )(own, low, high)


def join_half(whole, got, which):
    half = whole.shape[0] // 2

    def body(mine_ref, got_ref, out_ref):
        out_ref[...] = mine_ref[...] + got_ref[...].astype(jnp.float32)

    return pl.pallas_call(
        body,
        grid=(2,),
        in_specs=[
            pl.BlockSpec((half // 2, whole.shape[1]), lambda i: (2 * which + i, 0)),
            pl.BlockSpec((half // 2, whole.shape[1]), lambda i: (i, 0)),
        ],
        out_specs=pl.BlockSpec((half // 2, whole.shape[1]), lambda i: (2 * which + i, 0)),
        out_shape=jax.ShapeDtypeStruct(whole.shape, whole.dtype),
        input_output_aliases={0: 0},
        compiler_params=room(6),
        cost_estimate=cost(got.size, got.size * 10),
    )(whole, got)


def across(field, matrix_tile):
    return lax.dot_general(
        field, matrix_tile, (((1,), (1,)), ((), ())), preferred_element_type=jnp.float32
    )


def field_spec(rhs_count, sep_size):
    return pl.BlockSpec((1, rhs_count, sep_size), lambda f, i: (f, 0, 0))


def tile_spec(rhs_count):
    return pl.BlockSpec((1, rhs_count, TILE), lambda f, i: (f, 0, i))


def matrix_spec(sep_size):
    return pl.BlockSpec((1, TILE, sep_size), lambda f, i: (f, i, 0))


def first_solve(sep_rhs, parts, matrix):
    f_local, sep_size, _ = matrix.shape
    rhs_count = sep_rhs.shape[2]

    def body(rhs_ref, *rest):
        parts_refs, (matrix_ref, right_ref, out_ref, sent_ref, field) = rest[:6], rest[6:]
        f, i = pl.program_id(0), pl.program_id(1)
        for g in range(2):

            @pl.when((i == 0) & (f == g))
            def _(g=g):
                here, low, high = parts_refs[3 * g : 3 * g + 3]
                right = rhs_ref[0].astype(jnp.float32).T - (here[...] + low[...] + high[...])
                right_ref[0] = right
                field[...] = right.astype(jnp.bfloat16)

        out = across(field[...], matrix_ref[0])
        out_ref[0] = out
        sent_ref[0] = out.astype(jnp.bfloat16)

    whole = pl.BlockSpec((rhs_count, sep_size), lambda f, i: (0, 0))
    shape = (f_local, rhs_count, sep_size)
    return pl.pallas_call(
        body,
        grid=(f_local, sep_size // TILE),
        in_specs=[pl.BlockSpec((1, sep_size, rhs_count), lambda f, i: (f, 0, 0))]
        + [whole] * 6
        + [matrix_spec(sep_size)],
        out_specs=[field_spec(rhs_count, sep_size), tile_spec(rhs_count), tile_spec(rhs_count)],
        out_shape=[
            jax.ShapeDtypeStruct(shape, jnp.float32),
            jax.ShapeDtypeStruct(shape, jnp.float32),
            jax.ShapeDtypeStruct(shape, jnp.bfloat16),
        ],
        scratch_shapes=[pltpu.VMEM((rhs_count, sep_size), jnp.bfloat16)],
        compiler_params=room(16),
        cost_estimate=cost(2 * matrix.size * rhs_count, matrix.size * 2 + sep_rhs.size * 24),
    )(sep_rhs, *parts, matrix)


def residual_of(right_ref, mine_ref, coupling_ref, around):
    residual = right_ref[0] - mine_ref[0]
    for d in range(4):
        residual = residual + coupling_ref[0, d : d + 1, :] * around[d][0].astype(jnp.float32)
    return residual


def sweep(right_side, mine, around, coupling, matrix):
    f_local, sep_size, _ = matrix.shape
    rhs_count = mine.shape[1]

    def body(right_ref, whole_ref, *rest):
        around_refs, (coupling_ref, matrix_ref, mine_ref, out_ref, sent_ref, field) = rest[:4], rest[4:]

        @pl.when(pl.program_id(1) == 0)
        def _():
            field[...] = residual_of(right_ref, whole_ref, coupling_ref, around_refs).astype(jnp.bfloat16)

        out = mine_ref[0] + across(field[...], matrix_ref[0])
        out_ref[0] = out
        sent_ref[0] = out.astype(jnp.bfloat16)

    return pl.pallas_call(
        body,
        grid=(f_local, sep_size // TILE),
        in_specs=[field_spec(rhs_count, sep_size)] * 6
        + [pl.BlockSpec((1, 4, sep_size), lambda f, i: (f, 0, 0)), matrix_spec(sep_size), tile_spec(rhs_count)],
        out_specs=[tile_spec(rhs_count)] * 2,
        out_shape=[
            jax.ShapeDtypeStruct(mine.shape, jnp.float32),
            jax.ShapeDtypeStruct(mine.shape, jnp.bfloat16),
        ],
        scratch_shapes=[pltpu.VMEM((rhs_count, sep_size), jnp.bfloat16)],
        compiler_params=room(12),
        cost_estimate=cost(2 * matrix.size * rhs_count, matrix.size * 2 + mine.size * 24),
    )(right_side, mine, *around, coupling, matrix, mine)


def last_residual(weights, right_side, mine, around, coupling, copies):
    f_local, rhs_count, sep_size = mine.shape

    def body(weight_ref, right_ref, mine_ref, *rest):
        around_refs, (coupling_ref, field_ref, sum_ref, total) = rest[:4], rest[4:]
        f = pl.program_id(0)
        residual = residual_of(right_ref, mine_ref, coupling_ref, around_refs)
        field_ref[0] = residual.astype(jnp.bfloat16)
        square = jnp.sum(residual * residual, axis=0, keepdims=True) * weight_ref[f]

        @pl.when(f == 0)
        def _():
            total[...] = square

        @pl.when(f > 0)
        def _():
            total[...] += square

        @pl.when(f == f_local - 1)
        def _():
            sum_ref[...] = jnp.broadcast_to(jnp.sum(total[...]), sum_ref.shape)

    spec = pl.BlockSpec((1, rhs_count, sep_size), lambda f, *_: (f, 0, 0))
    return pl.pallas_call(
        body,
        grid_spec=pltpu.PrefetchScalarGridSpec(
            num_scalar_prefetch=1,
            grid=(f_local,),
            in_specs=[spec] * 6 + [pl.BlockSpec((1, 4, sep_size), lambda f, *_: (f, 0, 0))],
            out_specs=[spec, pl.BlockSpec((copies, 8, 128), lambda f, *_: (0, 0, 0))],
            scratch_shapes=[pltpu.VMEM((1, sep_size), jnp.float32)],
        ),
        out_shape=[
            jax.ShapeDtypeStruct(mine.shape, jnp.bfloat16),
            jax.ShapeDtypeStruct((copies, 8, 128), jnp.float32),
        ],
        compiler_params=room(12),
        cost_estimate=cost(mine.size * 12, mine.size * 18),
    )(weights, right_side, mine, *around, coupling)


def last_solve(mine, field, matrix):
    f_local, sep_size, _ = matrix.shape
    rhs_count = mine.shape[1]

    def body(mine_ref, field_ref, matrix_ref, out_ref):
        out_ref[0] = mine_ref[0].T + across(matrix_ref[0], field_ref[0])

    return pl.pallas_call(
        body,
        grid=(f_local, sep_size // TILE),
        in_specs=[tile_spec(rhs_count), field_spec(rhs_count, sep_size), matrix_spec(sep_size)],
        out_specs=pl.BlockSpec((1, TILE, rhs_count), lambda f, i: (f, i, 0)),
        out_shape=jax.ShapeDtypeStruct((f_local, sep_size, rhs_count), jnp.float32),
        compiler_params=room(10),
        cost_estimate=cost(2 * matrix.size * rhs_count, matrix.size * 2 + mine.size * 10),
    )(mine, field, matrix)


def turn(x, axis, by):
    return lax.ppermute(x, axis, [(i, (i + by) % SIDE) for i in range(SIDE)])


def neighbours(x, axis, count):
    up = [(i, i + 1) for i in range(count - 1)]
    return (lax.ppermute(x, axis, up), lax.ppermute(x, axis, [(b, a) for a, b in up]))


def on_device(update_basis, update_coeff, owner, sep_rhs, coupling, frontal_inverse):
    f_local = update_basis.shape[0]
    sep_size = update_basis.shape[3]
    rhs_count = update_coeff.shape[3]
    columns, rows = lax.axis_size(SX), lax.axis_size("sy")
    place = jnp.stack([lax.axis_index("sx_0"), lax.axis_index("sx_1")]).astype(jnp.int32)
    owners = owner[:, 0]
    data = (owners, place, update_basis, update_coeff)

    axes = (SX, SX[::-1])
    plan = tuple((f, 2, (pair,)) for f in range(2) for pair in (LOW, HIGH))
    far = owner_products(plan, (jnp.bfloat16,) * 4, *data)
    got = [(turn(far[2 * f], axes[f][0], 1), turn(far[2 * f + 1], axes[f][0], -1)) for f in range(2)]

    plan = tuple(
        (f, ahead, (pair,)) for f in range(2) for ahead, pair in ((1, LOW), (3, HIGH))
    ) + tuple((f, ahead, (pair,)) for f in range(2) for ahead, pair in ((1, HIGH), (3, LOW)))
    dtypes = (jnp.float32,) * 4 + (jnp.bfloat16,) * 4
    near = owner_products(plan, dtypes, *data, skipped=(0,) * 4 + (1,) * 4)

    sums, joined = [], []
    for f in range(2):
        following = join(near[2 * f], got[f][0], near[4 + 2 * f])
        preceding = join(near[2 * f + 1], got[f][1], near[5 + 2 * f])
        joined += [following, preceding]
        sums.append((turn(following, axes[f][0], 1), turn(preceding, axes[f][0], -1)))
    plan = tuple((f, 0, (LOW, HIGH)) for f in range(2))
    own = owner_products(plan, (jnp.float32,) * 2, *data, after=tuple(joined))

    parts = []
    for f in range(2):
        here, following, preceding, one_way, other_way = row_totals(own[f], *sums[f])
        axis = axes[f][1]
        a, b = turn(one_way, axis, 1), turn(other_way, axis, -1)
        following = join_half(following, a, 0)
        preceding = join_half(preceding, b, 1)
        parts += [here, turn(following, axis, 1), turn(preceding, axis, -1)]

    matrix = frontal_inverse[:, 0, 0]
    coupling_rows = coupling[:, 0, 0]
    right_side, mine, sent = first_solve(sep_rhs[:, 0, 0], parts, matrix)
    for _ in range(SWEEPS - 1):
        around = neighbours(sent, SX, columns) + neighbours(sent, "sy", rows)
        mine, sent = sweep(right_side, mine, around, coupling_rows, matrix)
    around = neighbours(sent, SX, columns) + neighbours(sent, "sy", rows)
    freq_ids = lax.axis_index("freq") * f_local + jnp.arange(f_local, dtype=jnp.int32) + 1
    weights = freq_ids.astype(jnp.float32) ** 2
    group = ("sy", "freq")
    field, squares = last_residual(
        weights, right_side, mine, around, coupling_rows, lax.axis_size(group)
    )
    squares = jnp.sum(lax.all_to_all(squares, group, 0, 0, tiled=True), axis=0)
    squares = jnp.broadcast_to(squares, (columns, *squares.shape))
    squares = jnp.sum(lax.all_to_all(squares, SX, 0, 0, tiled=True), axis=0)
    weighted_sum = squares[0, 0]
    solution = last_solve(mine, field, matrix)
    entries = float(f_local * lax.axis_size("freq") * columns * rows * sep_size * rhs_count)
    residual_total = jnp.sqrt(weighted_sum / entries + 1e-06)
    return (solution[:, None, None], residual_total)


def solution(mesh):
    finer = Mesh(
        mesh.devices.reshape(SIDE, SIDE, mesh.shape["sy"], mesh.shape["freq"]),
        ("sx_0", "sx_1", "sy", "freq"),
    )
    return jax.shard_map(
        on_device,
        mesh=finer,
        in_specs=(
            P("freq", SX_SY, None, None),
            P("freq", SX_SY, None, None),
            P(SX_SY, None),
            P("freq", SX, "sy", None, None),
            P("freq", SX, "sy", None, None),
            P("freq", SX, "sy", None, None),
        ),
        out_specs=(P("freq", SX, "sy", None, None), P()),
        check_vma=False,
    )
```

time: 192 us -> 163 us (0.85)
  other arithmetic: 24.2 us -> 0.12 us
  waiting for transfers between devices: 36.4 us -> 51 us
  starting transfers between devices: 62.4 us -> 51 us
  between operations: 12.9 us -> 2.78 us
  blocking collectives: 13.1 us -> 22 us
  matrix products: 8.54 us -> 0 us
  Pallas kernels: 18.3 us -> 26.3 us
  local copies, waits for them, and re-layouts: 14 us -> 9.05 us
    ppermute x16, waiting for transfers between devices: 14.7 us -> 32.2 us  [turn(): return lax.ppermute(x, axis, [(i, (i + by) % SIDE) for i in range(SIDE)])]
    slice x14 -> x1, local copies, waits for them, and re-layouts: 11.6 us -> 0.52 us  [on_device(): weighted_sum = squares[0, 0]]
    all_to_all x1, blocking collectives: 13.1 us -> 22 us  [on_device(): squares = jnp.sum(lax.all_to_all(squares, group, 0, 0, tiled=True), axis=0)]
    dot_general x3 -> x0, matrix products: 8.54 us -> none  [apply_inverse(): jnp.einsum('fst,ftn->fsn', inverse_block, field.astype(jnp.bfloat16), pre...]
    scatter-add x4 -> x0, other arithmetic: 8.19 us -> none  [add_into(): return x.at[index].add(y)]
    pallas_call x2 -> x17, Pallas kernels: 18.3 us -> 26.3 us  [the longest x3 9.31 us: owner_products(): pl.pallas_call(body, grid_spec=pltpu.PrefetchScalarGridSpec(num_scalar_pr...]
    ppermute x1 -> x0, starting transfers between devices: 7.94 us -> none  [on_device(): spread = spread + lax.ppermute(spread, 'freq', [(0, 1), (1, 0)])]
    unnamed x28 -> x18, local copies, waits for them, and re-layouts: 0.08 us -> 7.91 us
  transfers between devices with their start and end apart: 26 -> 25, of which waited for: 13 -> 12; matrix products, arithmetic and copies ran while one was open for 13% -> 0% of each run, Pallas kernels for 7% -> 8%
where the time goes in v2:
time: 163 us; the launch traced here: 162 us
  starting transfers between devices  51 us (31%)
  waiting for transfers between devices  51 us (31%)
  Pallas kernels  26.3 us (16%)
  blocking collectives  22 us (13%)
  local copies, waits for them, and re-layouts  9.05 us (6%)
  between operations  2.78 us (2%)
    ppermute x16, waiting for transfers between devices, turn(): return lax.ppermute(x, axis, [(i, (i + by) % SIDE) for i in range(SIDE)])  32.2 us
    ppermute x16, starting transfers between devices, turn(): return lax.ppermute(x, axis, [(i, (i + by) % SIDE) for i in range(SIDE)])  22.3 us
    all_to_all x1, blocking collectives, on_device(): squares = jnp.sum(lax.all_to_all(squares, group, 0, 0, tiled=True), axis=0)  22 us
    ppermute x4, waiting for transfers between devices, neighbours(): lax.ppermute(x, axis, [(b, a) for a, b in up])  16.3 us
    ppermute x4, starting transfers between devices, neighbours(): lax.ppermute(x, axis, up)  13.2 us
    all_to_all x1, starting transfers between devices, on_device(): squares = jnp.sum(lax.all_to_all(squares, SX, 0, 0, tiled=True), axis=0)  10.3 us
    pallas_call x3, Pallas kernels, owner_products(): pl.pallas_call(body, grid_spec=pltpu.PrefetchScalarGridSpec(num_scalar_pr...  9.31 us
    unnamed x18, local copies, waits for them, and re-layouts  7.91 us
  transfers between devices with their start and end apart: 25, of which 12 were waited for; matrix products, arithmetic and copies ran while one was open for 0% of the time, Pallas kernels for 8%

profile of v2, /device:TPU:1, one launch (start us, length us, event | category | flops | bytes accessed | tf_op | source)
XLA Modules:
  0.0 162.2 jit_solution(17474615687811712679)
XLA Ops:
  0.7 2.2 %copy-done.2 = bf16[2,32,32,1024]{3,2,1,0:T(8,128)(2,1)S(1)} copy-done((bf16[2,32,32,1024]{3,2,1,0:T(8,128)(2,1)S(1)}, bf16[2,32,32,1024]{3,2,1,0:T(8,128)(2,1)}, u32[]{:S(2)}) %copy-start.2) | copy-done | bytes 4194328
  2.9 1.0 copy-done.3
  3.9 0.7 copy-done.8
  4.6 2.5 %shard_map.78 = (bf16[2,128,1024]{2,1,0:T(8,128)(2,1)S(1)}, bf16[2,128,1024]{2,1,0:T(8,128)(2,1)S(1)}, bf16[2,128,1024]{2,1,0:T(8,128)(2,1)S(1)}, bf16[2,128,1024]{2,1,0:T(8,128)(2,1)S(1)}) custom-call(s32[32]{0:T(128)S(1)} %bitcast.16, s32[2]{0:T(128)S(1)} %pad_add_fusion.place_ref, bf16[2,32,32,1024]{3,2,1,0:T(8,128)(2,1)S(1)} %copy-done.2, ...), custom_call_target="tpu_custom_call" | custom-call | flops 1073741824 | bytes 6291456 | tf_op jit(solution)/shard_map/pallas_call | solution.py:107
  7.2 3.4 %collective-permute-start.3 = (bf16[2,128,1024]{2,1,0:T(8,128)(2,1)S(1)}, bf16[2,128,1024]{2,1,0:T(8,128)(2,1)S(1)}, u32[]{:S(2)}, u32[]{:S(2)}) collective-permute-start(bf16[2,128,1024]{2,1,0:T(8,128)(2,1)S(1)} %get-tuple-element.43), channel_id=1, source_target_pairs={{0,48},{16,0},{32,16},{48,32},{1,49},{17,1},{33,17},{49,33},{2,50}... | collective-permute-start | bytes 1572872 | tf_op jit(solution)/shard_map/ppermute | solution.py:360
  10.5 2.7 %collective-permute-start.1 = (bf16[2,128,1024]{2,1,0:T(8,128)(2,1)S(1)}, bf16[2,128,1024]{2,1,0:T(8,128)(2,1)S(1)}, u32[]{:S(2)}, u32[]{:S(2)}) collective-permute-start(bf16[2,128,1024]{2,1,0:T(8,128)(2,1)S(1)} %get-tuple-element.37), channel_id=1, source_target_pairs={{0,192},{64,0},{128,64},{192,128},{1,193},{65,1},{129,65},{193,129... | collective-permute-start | bytes 1572872 | tf_op jit(solution)/shard_map/ppermute | solution.py:360
  13.3 4.2 %shard_map.77 = (f32[2,128,1024]{2,1,0:T(8,128)S(1)}, f32[2,128,1024]{2,1,0:T(8,128)S(1)}, f32[2,128,1024]{2,1,0:T(8,128)S(1)}, f32[2,128,1024]{2,1,0:T(8,128)S(...) custom-call(s32[32]{0:T(128)S(1)} %bitcast.17, ...), custom_call_target="tpu_custom_call" | custom-call | flops 2147483648 | bytes 10485760 | tf_op jit(solution)/shard_map/pallas_call | solution.py:107
  17.5 3.6 %collective-permute-done.3.got_ref = bf16[2,128,1024]{2,1,0:T(8,128)(2,1)S(1)} collective-permute-done((bf16[2,128,1024]{2,1,0:T(8,128)(2,1)S(1)}, bf16[2,128,1024]{2,1,0:T(8,128)(2,1)S(1)}, u32[]{:S(2)}, u32[]{:S(2)}) %collective-permute-start.3) | collective-permute-done | bytes 524320 | tf_op jit(solution)/shard_map/ppermute | solution.py:360
  21.3 3.5 %collective-permute-start.11 = (bf16[4,128,1024]{2,1,0:T(8,128)(2,1)S(1)}, bf16[4,128,1024]{2,1,0:T(8,128)(2,1)S(1)}, u32[]{:S(2)}, u32[]{:S(2)}) collective-permute-start(bf16[4,128,1024]{2,1,0:T(8,128)(2,1)S(1)} %shard_map.82.rest_3_), channel_id=1, source_target_pairs={{0,48},{16,0},{32,16},{48,32},{1,49},{17,1},{33,17},{49,33},{2,50}... | collective-permute-start | bytes 3145736 | tf_op jit(solution)/shard_map/ppermute | solution.py:360
  25.0 0.1 shard_map.80.rest_1_
  25.1 2.8 %collective-permute-start.5 = (bf16[4,128,1024]{2,1,0:T(8,128)(2,1)S(1)}, bf16[4,128,1024]{2,1,0:T(8,128)(2,1)S(1)}, u32[]{:S(2)}, u32[]{:S(2)}) collective-permute-start(bf16[4,128,1024]{2,1,0:T(8,128)(2,1)S(1)} %shard_map.80.rest_1_), channel_id=1, source_target_pairs={{0,192},{64,0},{128,64},{192,128},{1,193},{65,1},{129,65},{193,129... | collective-permute-start | bytes 3145736 | tf_op jit(solution)/shard_map/ppermute | solution.py:360
  28.2 2.5 %shard_map.83 = (f32[4,128,1024]{2,1,0:T(8,128)S(1)}, f32[4,128,1024]{2,1,0:T(8,128)S(1)}) custom-call(s32[32]{0:T(128)S(1)} %bitcast.18, s32[2]{0:T(128)S(1)} %pad_add_fusion.place_ref, bf16[2,32,32,1024]{3,2,1,0:T(8,128)(2,1)S(1)} %copy-done.2, bf16[2,32,32,128]{3,2,1,0:T(8,128)(2,1)S(1)} %copy-done.3, bf16[4,128,1024]{2,1,0:T(8,128)(2,1)S(1)} %shard_map.79.rest_0_, ...), custom_call_target="tpu_custom_call" | custom-call | flops 1073741824 | bytes 8388608 | tf_op jit(solution)/shard_map/pallas_call | solution.py:107
  30.7 15.0 %collective-permute-done.11.high_ref = bf16[4,128,1024]{2,1,0:T(8,128)(2,1)S(1)} collective-permute-done((bf16[4,128,1024]{2,1,0:T(8,128)(2,1)S(1)}, bf16[4,128,1024]{2,1,0:T(8,128)(2,1)S(1)}, u32[]{:S(2)}, u32[]{:S(2)}) %collective-permute-start.11) | collective-permute-done | bytes 1048608 | tf_op jit(solution)/shard_map/ppermute | solution.py:360
  45.7 3.3 %collective-permute-done.10.low_ref = bf16[4,128,1024]{2,1,0:T(8,128)(2,1)S(1)} collective-permute-done((bf16[4,128,1024]{2,1,0:T(8,128)(2,1)S(1)}, bf16[4,128,1024]{2,1,0:T(8,128)(2,1)S(1)}, u32[]{:S(2)}, u32[]{:S(2)}) %collective-permute-start.10) | collective-permute-done | bytes 1048608 | tf_op jit(solution)/shard_map/ppermute | solution.py:360
  49.1 0.9 shard_map.87
  50.0 2.8 %collective-permute-start.14 = (bf16[64,1024]{1,0:T(8,128)(2,1)S(1)}, bf16[64,1024]{1,0:T(8,128)(2,1)S(1)}, u32[]{:S(2)}, u32[]{:S(2)}) collective-permute-start(bf16[64,1024]{1,0:T(8,128)(2,1)S(1)} %get-tuple-element.56), channel_id=1, source_target_pairs={{0,192},{64,0},{128,64},{192,128},{1,193},{65,1},{129,65},{193,129... | collective-permute-start | bytes 393224 | tf_op jit(solution)/shard_map/ppermute | solution.py:360
  52.9 0.9 shard_map.84
  53.8 1.6 collective-permute-start.8
  55.4 2.7 %collective-permute-start.15 = (f32[128,1024]{1,0:T(8,128)S(1)}, f32[128,1024]{1,0:T(8,128)S(1)}, u32[]{:S(2)}, u32[]{:S(2)}) collective-permute-start(f32[128,1024]{1,0:T(8,128)S(1)} %shard_map.89), channel_id=1, source_target_pairs={{0,192},{64,0},{128,64},{192,128},{1,193},{65,1},{129,65},{193,129... | collective-permute-start | bytes 1572872 | tf_op jit(solution)/shard_map/ppermute | solution.py:360
  58.4 2.4 %collective-permute-start.9 = (f32[128,1024]{1,0:T(8,128)S(1)}, f32[128,1024]{1,0:T(8,128)S(1)}, u32[]{:S(2)}, u32[]{:S(2)}) collective-permute-start(f32[128,1024]{1,0:T(8,128)S(1)} %shard_map.86), channel_id=1, source_target_pairs={{0,48},{16,0},{32,16},{48,32},{1,49},{17,1},{33,17},{49,33},{2,50}... | collective-permute-start | bytes 1572872 | tf_op jit(solution)/shard_map/ppermute | solution.py:360
  61.0 4.7 %collective-permute-done.15.rest_5_ = f32[128,1024]{1,0:T(8,128)S(1)} collective-permute-done((f32[128,1024]{1,0:T(8,128)S(1)}, f32[128,1024]{1,0:T(8,128)S(1)}, u32[]{:S(2)}, u32[]{:S(2)}) %collective-permute-start.15) | collective-permute-done | bytes 524320 | tf_op jit(solution)/shard_map/ppermute | solution.py:360
  65.7 3.3 %collective-permute-done.13.rest_4_ = f32[128,1024]{1,0:T(8,128)S(1)} collective-permute-done((f32[128,1024]{1,0:T(8,128)S(1)}, f32[128,1024]{1,0:T(8,128)S(1)}, u32[]{:S(2)}, u32[]{:S(2)}) %collective-permute-start.13) | collective-permute-done | bytes 524320 | tf_op jit(solution)/shard_map/ppermute | solution.py:360
  68.9 2.2 %collective-permute-done.7.rest_1_ = f32[128,1024]{1,0:T(8,128)S(1)} collective-permute-done((f32[128,1024]{1,0:T(8,128)S(1)}, f32[128,1024]{1,0:T(8,128)S(1)}, u32[]{:S(2)}, u32[]{:S(2)}) %collective-permute-start.7) | collective-permute-done | bytes 524320 | tf_op jit(solution)/shard_map/ppermute | solution.py:360
  71.1 3.1 %shard_map.90 = (f32[2,128,1024]{2,1,0:T(8,128)S(1)}, f32[2,128,1024]{2,1,0:T(8,128)S(1)}, bf16[2,128,1024]{2,1,0:T(8,128)(2,1)S(1)}) custom-call(bf16[2,1024,128]{2,1,0:T(8,128)(2,1)S(1)} %bitcast.13, f32[128,1024]{1,0:T(8,128)S(1)} %get-tuple-element.46.rest_0_, f32[128,1024]{1,0:T(8,128)S(1)} %collective-permute-done.7.rest_1_, ...), custom_call_target="tpu_custom_call" | custom-call | flops 536870912 | bytes 10485760 | tf_op jit(solution)/shard_map/pallas_call | solution.py:244
  74.3 1.3 collective-permute-start.16
  75.6 1.3 collective-permute-start.17
  76.9 3.6 %collective-permute-start.18 = (bf16[2,128,1024]{2,1,0:T(8,128)(2,1)S(1)}, bf16[2,128,1024]{2,1,0:T(8,128)(2,1)S(1)}, u32[]{:S(2)}, u32[]{:S(2)}) collective-permute-start(bf16[2,128,1024]{2,1,0:T(8,128)(2,1)S(1)} %get-tuple-element.59), channel_id=1, source_target_pairs={{0,2},{2,4},{4,6},{6,8},{8,10},{10,12},{12,14},{1,3},{3,5},{5,7},{... | collective-permute-start | bytes 1572872 | tf_op jit(solution)/shard_map/ppermute | solution.py:365
  80.5 1.3 collective-permute-start.19
  81.8 3.7 %collective-permute-done.17.rest_1_ = bf16[2,128,1024]{2,1,0:T(8,128)(2,1)S(1)} collective-permute-done((bf16[2,128,1024]{2,1,0:T(8,128)(2,1)S(1)}, bf16[2,128,1024]{2,1,0:T(8,128)(2,1)S(1)}, u32[]{:S(2)}, u32[]{:S(2)}) %collective-permute-start.17) | collective-permute-done | bytes 524320 | tf_op jit(solution)/shard_map/ppermute | solution.py:365
  85.5 1.0 collective-permute-done.18.rest_2_
  86.6 4.3 %collective-permute-done.19.rest_3_ = bf16[2,128,1024]{2,1,0:T(8,128)(2,1)S(1)} collective-permute-done((bf16[2,128,1024]{2,1,0:T(8,128)(2,1)S(1)}, bf16[2,128,1024]{2,1,0:T(8,128)(2,1)S(1)}, u32[]{:S(2)}, u32[]{:S(2)}) %collective-permute-start.19) | collective-permute-done | bytes 524320 | tf_op jit(solution)/shard_map/ppermute | solution.py:365
  90.9 4.7 %shard_map.91 = (f32[2,128,1024]{2,1,0:T(8,128)S(1)}, bf16[2,128,1024]{2,1,0:T(8,128)(2,1)}) custom-call(f32[2,128,1024]{2,1,0:T(8,128)S(1)} %get-tuple-element.57.right_ref, f32[2,128,1024]{2,1,0:T(8,128)S(1)} %get-tuple-element.58.whole_ref.rest_6_, bf16[2,128,1024]{2,1,0:T(8,128)(2,1)S(1)} %collective-permute-done.16.rest_0_, ...), custom_call_target="tpu_custom_call" | custom-call | flops 536870912 | bytes 10485760 | tf_op jit(solution)/shard_map/pallas_call | solution.py:284
  95.6 3.7 %collective-permute-start.20 = (bf16[2,128,1024]{2,1,0:T(8,128)(2,1)}, bf16[2,128,1024]{2,1,0:T(8,128)(2,1)S(1)}, u32[]{:S(2)}, u32[]{:S(2)}) collective-permute-start(bf16[2,128,1024]{2,1,0:T(8,128)(2,1)} %get-tuple-element.61), channel_id=1, source_target_pairs={{0,16},{16,32},{32,48},{48,64},{64,80},{80,96},{96,112},{112,128},... | collective-permute-start | bytes 1572872 | tf_op jit(solution)/shard_map/ppermute | solution.py:365
  99.3 1.3 collective-permute-start.21
  100.6 4.6 %collective-permute-start.22 = (bf16[2,128,1024]{2,1,0:T(8,128)(2,1)}, bf16[2,128,1024]{2,1,0:T(8,128)(2,1)}, u32[]{:S(2)}, u32[]{:S(2)}) collective-permute-start(bf16[2,128,1024]{2,1,0:T(8,128)(2,1)} %get-tuple-element.61), channel_id=1, source_target_pairs={{0,2},{2,4},{4,6},{6,8},{8,10},{10,12},{12,14},{1,3},{3,5},{5,7},{... | collective-permute-start | bytes 1572872 | tf_op jit(solution)/shard_map/ppermute | solution.py:365
  105.2 1.3 collective-permute-start.23
  106.5 2.9 %collective-permute-done.21.rest_1_ = bf16[2,128,1024]{2,1,0:T(8,128)(2,1)S(1)} collective-permute-done((bf16[2,128,1024]{2,1,0:T(8,128)(2,1)}, bf16[2,128,1024]{2,1,0:T(8,128)(2,1)S(1)}, u32[]{:S(2)}, u32[]{:S(2)}) %collective-permute-start.21) | collective-permute-done | bytes 524320 | tf_op jit(solution)/shard_map/ppermute | solution.py:365
  109.4 1.4 collective-permute-done.22.rest_2_
  110.8 5.4 %collective-permute-done.23.rest_3_ = bf16[2,128,1024]{2,1,0:T(8,128)(2,1)} collective-permute-done((bf16[2,128,1024]{2,1,0:T(8,128)(2,1)}, bf16[2,128,1024]{2,1,0:T(8,128)(2,1)}, u32[]{:S(2)}, u32[]{:S(2)}) %collective-permute-start.23) | collective-permute-done | bytes 524320 | tf_op jit(solution)/shard_map/ppermute | solution.py:365
  116.3 2.3 %shard_map.92 = (bf16[2,128,1024]{2,1,0:T(8,128)(2,1)S(1)}, f32[16,8,128]{2,1,0:T(8,128)S(1)}) custom-call(f32[2]{0:T(128)S(1)} %convert_multiply_fusion.weight_ref, f32[2,128,1024]{2,1,0:T(8,128)S(1)} %get-tuple-element.57.right_ref, f32[2,128,1024]{2,1,0:T(8,128)S(1)} %get-tuple-element.60.mine_ref, ...), custom_call_target="tpu_custom_call" | custom-call | flops 3145728 | bytes 4718592 | tf_op jit(solution)/shard_map/pallas_call | solution.py:323
  118.6 0.8 copy-done.4
  119.4 22.0 %all_to_all.10 = f32[16,8,128]{2,1,0:T(8,128)S(1)} all-to-all(f32[16,8,128]{2,1,0:T(8,128)S(1)} %get-tuple-element.63), channel_id=1, replica_groups=mesh['sx_0'=4,'sx_1'=4,'sy'=8,'freq'=2] {'sy','freq'}, dimensions={0} | all-to-all | bytes 131072 | tf_op jit(solution)/shard_map/all_to_all | solution.py:419
  141.4 0.6 broadcast_in_dim.7
  142.1 10.3 %all-to-all-start.1 = ((f32[16,8,128]{2,1,0:T(8,128)}), f32[16,8,128]{2,1,0:T(8,128)S(1)}, u32[]{:S(2)}, u32[]{:S(2)}) async-start(f32[16,8,128]{2,1,0:T(8,128)} %broadcast_in_dim.7), calls=%async_computation.1 | async-start | bytes 131072 | tf_op jit(solution)/shard_map/all_to_all | solution.py:421
  152.4 2.2 %copy-done.1 = bf16[2,1,1,1024,1024]{4,3,2,1,0:T(8,128)(2,1)S(1)} copy-done((bf16[2,1,1,1024,1024]{4,3,2,1,0:T(8,128)(2,1)S(1)}, bf16[2,1,1,1024,1024]{4,3,2,1,0:T(8,128)(2,1)}, u32[]{:S(2)}) %copy-start.1) | copy-done | bytes 4194328
  154.6 1.0 copy-done.5
  155.6 4.3 %shard_map.93 = f32[2,1024,128]{2,1,0:T(8,128)} custom-call(f32[2,128,1024]{2,1,0:T(8,128)S(1)} %get-tuple-element.60.mine_ref, bf16[2,128,1024]{2,1,0:T(8,128)(2,1)S(1)} %copy-done.5, bf16[2,1024,1024]{2,1,0:T(8,128)(2,1)S(1)} %bitcast.12), custom_call_target="tpu_custom_call" | custom-call | flops 536870912 | bytes 6815744 | tf_op jit(solution)/shard_map/pallas_call | solution.py:348
  159.9 0.5 slice.3
  (44 shorter events, 1.1 us)
Async XLA Ops:
  0.7 2.2 %copy-start.2 = (bf16[2,32,32,1024]{3,2,1,0:T(8,128)(2,1)S(1)}, bf16[2,32,32,1024]{3,2,1,0:T(8,128)(2,1)}, u32[]{:S(2)}) copy-start(bf16[2,32,32,1024]{3,2,1,0:T(8,128)(2,1)} %basis_ref.5) | copy-start | bytes 12582916
  2.9 1.0 copy-start.3
  3.9 0.7 copy-start.8
  7.2 14.0 %collective-permute-start.3 = (bf16[2,128,1024]{2,1,0:T(8,128)(2,1)S(1)}, bf16[2,128,1024]{2,1,0:T(8,128)(2,1)S(1)}, u32[]{:S(2)}, u32[]{:S(2)}) collective-permute-start(bf16[2,128,1024]{2,1,0:T(8,128)(2,1)S(1)} %get-tuple-element.43), channel_id=1, source_target_pairs={{0,48},{16,0},{32,16},{48,32},{1,49},{17,1},{33,17},{49,33},{2,50}... | collective-permute-start | bytes 1572872 | tf_op jit(solution)/shard_map/ppermute | solution.py:360
  10.5 14.2 %collective-permute-start.2 = (bf16[2,128,1024]{2,1,0:T(8,128)(2,1)S(1)}, bf16[2,128,1024]{2,1,0:T(8,128)(2,1)S(1)}, u32[]{:S(2)}, u32[]{:S(2)}) collective-permute-start(bf16[2,128,1024]{2,1,0:T(8,128)(2,1)S(1)} %get-tuple-element.40), channel_id=1, source_target_pairs={{0,16},{16,32},{32,48},{48,0},{1,17},{17,33},{33,49},{49,1},{2,18}... | collective-permute-start | bytes 1572872 | tf_op jit(solution)/shard_map/ppermute | solution.py:360
  10.5 14.4 %collective-permute-start.1 = (bf16[2,128,1024]{2,1,0:T(8,128)(2,1)S(1)}, bf16[2,128,1024]{2,1,0:T(8,128)(2,1)S(1)}, u32[]{:S(2)}, u32[]{:S(2)}) collective-permute-start(bf16[2,128,1024]{2,1,0:T(8,128)(2,1)S(1)} %get-tuple-element.37), channel_id=1, source_target_pairs={{0,192},{64,0},{128,64},{192,128},{1,193},{65,1},{129,65},{193,129... | collective-permute-start | bytes 1572872 | tf_op jit(solution)/shard_map/ppermute | solution.py:360
  13.3 14.7 %collective-permute-start = (bf16[2,128,1024]{2,1,0:T(8,128)(2,1)S(1)}, bf16[2,128,1024]{2,1,0:T(8,128)(2,1)S(1)}, u32[]{:S(2)}, u32[]{:S(2)}) collective-permute-start(bf16[2,128,1024]{2,1,0:T(8,128)(2,1)S(1)} %get-tuple-element.34), channel_id=1, source_target_pairs={{0,64},{64,128},{128,192},{192,0},{1,65},{65,129},{129,193},{193,1... | collective-permute-start | bytes 1572872 | tf_op jit(solution)/shard_map/ppermute | solution.py:360
  21.3 24.5 %collective-permute-start.11 = (bf16[4,128,1024]{2,1,0:T(8,128)(2,1)S(1)}, bf16[4,128,1024]{2,1,0:T(8,128)(2,1)S(1)}, u32[]{:S(2)}, u32[]{:S(2)}) collective-permute-start(bf16[4,128,1024]{2,1,0:T(8,128)(2,1)S(1)} %shard_map.82.rest_3_), channel_id=1, source_target_pairs={{0,48},{16,0},{32,16},{48,32},{1,49},{17,1},{33,17},{49,33},{2,50}... | collective-permute-start | bytes 3145736 | tf_op jit(solution)/shard_map/ppermute | solution.py:360
  24.9 24.2 %collective-permute-start.10 = (bf16[4,128,1024]{2,1,0:T(8,128)(2,1)S(1)}, bf16[4,128,1024]{2,1,0:T(8,128)(2,1)S(1)}, u32[]{:S(2)}, u32[]{:S(2)}) collective-permute-start(bf16[4,128,1024]{2,1,0:T(8,128)(2,1)S(1)} %shard_map.81.rest_2_), channel_id=1, source_target_pairs={{0,16},{16,32},{32,48},{48,0},{1,17},{17,33},{33,49},{49,1},{2,18}... | collective-permute-start | bytes 3145736 | tf_op jit(solution)/shard_map/ppermute | solution.py:360
  25.1 27.7 %collective-permute-start.5 = (bf16[4,128,1024]{2,1,0:T(8,128)(2,1)S(1)}, bf16[4,128,1024]{2,1,0:T(8,128)(2,1)S(1)}, u32[]{:S(2)}, u32[]{:S(2)}) collective-permute-start(bf16[4,128,1024]{2,1,0:T(8,128)(2,1)S(1)} %shard_map.80.rest_1_), channel_id=1, source_target_pairs={{0,192},{64,0},{128,64},{192,128},{1,193},{65,1},{129,65},{193,129... | collective-permute-start | bytes 3145736 | tf_op jit(solution)/shard_map/ppermute | solution.py:360
  28.1 24.8 %collective-permute-start.4 = (bf16[4,128,1024]{2,1,0:T(8,128)(2,1)S(1)}, bf16[4,128,1024]{2,1,0:T(8,128)(2,1)S(1)}, u32[]{:S(2)}, u32[]{:S(2)}) collective-permute-start(bf16[4,128,1024]{2,1,0:T(8,128)(2,1)S(1)} %shard_map.79.rest_0_), channel_id=1, source_target_pairs={{0,64},{64,128},{128,192},{192,0},{1,65},{65,129},{129,193},{193,1... | collective-permute-start | bytes 3145736 | tf_op jit(solution)/shard_map/ppermute | solution.py:360
  50.0 5.4 %collective-permute-start.14 = (bf16[64,1024]{1,0:T(8,128)(2,1)S(1)}, bf16[64,1024]{1,0:T(8,128)(2,1)S(1)}, u32[]{:S(2)}, u32[]{:S(2)}) collective-permute-start(bf16[64,1024]{1,0:T(8,128)(2,1)S(1)} %get-tuple-element.56), channel_id=1, source_target_pairs={{0,192},{64,0},{128,64},{192,128},{1,193},{65,1},{129,65},{193,129... | collective-permute-start | bytes 393224 | tf_op jit(solution)/shard_map/ppermute | solution.py:360
  52.8 5.3 %collective-permute-start.12 = (bf16[64,1024]{1,0:T(8,128)(2,1)S(1)}, bf16[64,1024]{1,0:T(8,128)(2,1)S(1)}, u32[]{:S(2)}, u32[]{:S(2)}) collective-permute-start(bf16[64,1024]{1,0:T(8,128)(2,1)S(1)} %get-tuple-element.54), channel_id=1, source_target_pairs={{0,64},{64,128},{128,192},{192,0},{1,65},{65,129},{129,193},{193,1... | collective-permute-start | bytes 393224 | tf_op jit(solution)/shard_map/ppermute | solution.py:360
  52.8 18.3 %copy-start = (bf16[2,1,1,1024,1024]{4,3,2,1,0:T(8,128)(2,1)S(1)}, bf16[2,1,1,1024,1024]{4,3,2,1,0:T(8,128)(2,1)}, u32[]{:S(2)}) copy-start(bf16[2,1,1,1024,1024]{4,3,2,1,0:T(8,128)(2,1)} %param.11) | copy-start | bytes 12582916
  52.8 18.3 %copy-start.6 = (bf16[2,1,1,1024,128]{4,3,2,1,0:T(8,128)(2,1)S(1)}, bf16[2,1,1,1024,128]{4,3,2,1,0:T(8,128)(2,1)}, u32[]{:S(2)}) copy-start(bf16[2,1,1,1024,128]{4,3,2,1,0:T(8,128)(2,1)} %param.9) | copy-start | bytes 1572868
  53.8 4.5 %collective-permute-start.8 = (bf16[64,1024]{1,0:T(8,128)(2,1)S(1)}, bf16[64,1024]{1,0:T(8,128)(2,1)S(1)}, u32[]{:S(2)}, u32[]{:S(2)}) collective-permute-start(bf16[64,1024]{1,0:T(8,128)(2,1)S(1)} %get-tuple-element.50), channel_id=1, source_target_pairs={{0,48},{16,0},{32,16},{48,32},{1,49},{17,1},{33,17},{49,33},{2,50}... | collective-permute-start | bytes 393224 | tf_op jit(solution)/shard_map/ppermute | solution.py:360
  55.4 5.5 %collective-permute-start.6 = (bf16[64,1024]{1,0:T(8,128)(2,1)S(1)}, bf16[64,1024]{1,0:T(8,128)(2,1)S(1)}, u32[]{:S(2)}, u32[]{:S(2)}) collective-permute-start(bf16[64,1024]{1,0:T(8,128)(2,1)S(1)} %get-tuple-element.48), channel_id=1, source_target_pairs={{0,16},{16,32},{32,48},{48,0},{1,17},{17,33},{33,49},{49,1},{2,18}... | collective-permute-start | bytes 393224 | tf_op jit(solution)/shard_map/ppermute | solution.py:360
  55.4 10.2 %collective-permute-start.15 = (f32[128,1024]{1,0:T(8,128)S(1)}, f32[128,1024]{1,0:T(8,128)S(1)}, u32[]{:S(2)}, u32[]{:S(2)}) collective-permute-start(f32[128,1024]{1,0:T(8,128)S(1)} %shard_map.89), channel_id=1, source_target_pairs={{0,192},{64,0},{128,64},{192,128},{1,193},{65,1},{129,65},{193,129... | collective-permute-start | bytes 1572872 | tf_op jit(solution)/shard_map/ppermute | solution.py:360
  58.2 10.7 %collective-permute-start.13 = (f32[128,1024]{1,0:T(8,128)S(1)}, f32[128,1024]{1,0:T(8,128)S(1)}, u32[]{:S(2)}, u32[]{:S(2)}) collective-permute-start(f32[128,1024]{1,0:T(8,128)S(1)} %shard_map.88), channel_id=1, source_target_pairs={{0,64},{64,128},{128,192},{192,0},{1,65},{65,129},{129,193},{193,1... | collective-permute-start | bytes 1572872 | tf_op jit(solution)/shard_map/ppermute | solution.py:360
  58.4 10.5 %collective-permute-start.9 = (f32[128,1024]{1,0:T(8,128)S(1)}, f32[128,1024]{1,0:T(8,128)S(1)}, u32[]{:S(2)}, u32[]{:S(2)}) collective-permute-start(f32[128,1024]{1,0:T(8,128)S(1)} %shard_map.86), channel_id=1, source_target_pairs={{0,48},{16,0},{32,16},{48,32},{1,49},{17,1},{33,17},{49,33},{2,50}... | collective-permute-start | bytes 1572872 | tf_op jit(solution)/shard_map/ppermute | solution.py:360
  60.9 30.0 %copy-start.7 = (f32[2,1,1,4,1024]{4,3,2,1,0:T(4,128)S(1)}, f32[2,1,1,4,1024]{4,3,2,1,0:T(4,128)}, u32[]{:S(2)}) copy-start(f32[2,1,1,4,1024]{4,3,2,1,0:T(4,128)} %param.10) | copy-start | bytes 98308
  60.9 10.2 %collective-permute-start.7 = (f32[128,1024]{1,0:T(8,128)S(1)}, f32[128,1024]{1,0:T(8,128)S(1)}, u32[]{:S(2)}, u32[]{:S(2)}) collective-permute-start(f32[128,1024]{1,0:T(8,128)S(1)} %shard_map.85), channel_id=1, source_target_pairs={{0,16},{16,32},{32,48},{48,0},{1,17},{17,33},{33,49},{49,1},{2,18}... | collective-permute-start | bytes 1572872 | tf_op jit(solution)/shard_map/ppermute | solution.py:360
  74.3 7.5 %collective-permute-start.16 = (bf16[2,128,1024]{2,1,0:T(8,128)(2,1)S(1)}, bf16[2,128,1024]{2,1,0:T(8,128)(2,1)S(1)}, u32[]{:S(2)}, u32[]{:S(2)}) collective-permute-start(bf16[2,128,1024]{2,1,0:T(8,128)(2,1)S(1)} %get-tuple-element.59), channel_id=1, source_target_pairs={{0,16},{16,32},{32,48},{48,64},{64,80},{80,96},{96,112},{112,128},... | collective-permute-start | bytes 1572872 | tf_op jit(solution)/shard_map/ppermute | solution.py:365
  75.6 9.9 %collective-permute-start.17 = (bf16[2,128,1024]{2,1,0:T(8,128)(2,1)S(1)}, bf16[2,128,1024]{2,1,0:T(8,128)(2,1)S(1)}, u32[]{:S(2)}, u32[]{:S(2)}) collective-permute-start(bf16[2,128,1024]{2,1,0:T(8,128)(2,1)S(1)} %get-tuple-element.59), channel_id=1, source_target_pairs={{16,0},{32,16},{48,32},{64,48},{80,64},{96,80},{112,96},{128,112},... | collective-permute-start | bytes 1572872 | tf_op jit(solution)/shard_map/ppermute | solution.py:365
  76.9 9.7 %collective-permute-start.18 = (bf16[2,128,1024]{2,1,0:T(8,128)(2,1)S(1)}, bf16[2,128,1024]{2,1,0:T(8,128)(2,1)S(1)}, u32[]{:S(2)}, u32[]{:S(2)}) collective-permute-start(bf16[2,128,1024]{2,1,0:T(8,128)(2,1)S(1)} %get-tuple-element.59), channel_id=1, source_target_pairs={{0,2},{2,4},{4,6},{6,8},{8,10},{10,12},{12,14},{1,3},{3,5},{5,7},{... | collective-permute-start | bytes 1572872 | tf_op jit(solution)/shard_map/ppermute | solution.py:365
  80.5 10.4 %collective-permute-start.19 = (bf16[2,128,1024]{2,1,0:T(8,128)(2,1)S(1)}, bf16[2,128,1024]{2,1,0:T(8,128)(2,1)S(1)}, u32[]{:S(2)}, u32[]{:S(2)}) collective-permute-start(bf16[2,128,1024]{2,1,0:T(8,128)(2,1)S(1)} %get-tuple-element.59), channel_id=1, source_target_pairs={{2,0},{4,2},{6,4},{8,6},{10,8},{12,10},{14,12},{3,1},{5,3},{7,5},{... | collective-permute-start | bytes 1572872 | tf_op jit(solution)/shard_map/ppermute | solution.py:365
  95.6 11.0 %collective-permute-start.20 = (bf16[2,128,1024]{2,1,0:T(8,128)(2,1)}, bf16[2,128,1024]{2,1,0:T(8,128)(2,1)S(1)}, u32[]{:S(2)}, u32[]{:S(2)}) collective-permute-start(bf16[2,128,1024]{2,1,0:T(8,128)(2,1)} %get-tuple-element.61), channel_id=1, source_target_pairs={{0,16},{16,32},{32,48},{48,64},{64,80},{80,96},{96,112},{112,128},... | collective-permute-start | bytes 1572872 | tf_op jit(solution)/shard_map/ppermute | solution.py:365
  99.3 10.1 %collective-permute-start.21 = (bf16[2,128,1024]{2,1,0:T(8,128)(2,1)}, bf16[2,128,1024]{2,1,0:T(8,128)(2,1)S(1)}, u32[]{:S(2)}, u32[]{:S(2)}) collective-permute-start(bf16[2,128,1024]{2,1,0:T(8,128)(2,1)} %get-tuple-element.61), channel_id=1, source_target_pairs={{16,0},{32,16},{48,32},{64,48},{80,64},{96,80},{112,96},{128,112},... | collective-permute-start | bytes 1572872 | tf_op jit(solution)/shard_map/ppermute | solution.py:365
  100.6 10.3 %collective-permute-start.22 = (bf16[2,128,1024]{2,1,0:T(8,128)(2,1)}, bf16[2,128,1024]{2,1,0:T(8,128)(2,1)}, u32[]{:S(2)}, u32[]{:S(2)}) collective-permute-start(bf16[2,128,1024]{2,1,0:T(8,128)(2,1)} %get-tuple-element.61), channel_id=1, source_target_pairs={{0,2},{2,4},{4,6},{6,8},{8,10},{10,12},{12,14},{1,3},{3,5},{5,7},{... | collective-permute-start | bytes 1572872 | tf_op jit(solution)/shard_map/ppermute | solution.py:365
  105.2 11.0 %collective-permute-start.23 = (bf16[2,128,1024]{2,1,0:T(8,128)(2,1)}, bf16[2,128,1024]{2,1,0:T(8,128)(2,1)}, u32[]{:S(2)}, u32[]{:S(2)}) collective-permute-start(bf16[2,128,1024]{2,1,0:T(8,128)(2,1)} %get-tuple-element.61), channel_id=1, source_target_pairs={{2,0},{4,2},{6,4},{8,6},{10,8},{12,10},{14,12},{3,1},{5,3},{7,5},{... | collective-permute-start | bytes 1572872 | tf_op jit(solution)/shard_map/ppermute | solution.py:365
  118.6 0.8 copy-start.4
  142.1 17.8 %all-to-all-start.1 = ((f32[16,8,128]{2,1,0:T(8,128)}), f32[16,8,128]{2,1,0:T(8,128)S(1)}, u32[]{:S(2)}, u32[]{:S(2)}) async-start(f32[16,8,128]{2,1,0:T(8,128)} %broadcast_in_dim.7), calls=%async_computation.1 | async-start | bytes 131072 | tf_op jit(solution)/shard_map/all_to_all | solution.py:421
  152.4 2.2 %copy-start.1 = (bf16[2,1,1,1024,1024]{4,3,2,1,0:T(8,128)(2,1)S(1)}, bf16[2,1,1,1024,1024]{4,3,2,1,0:T(8,128)(2,1)}, u32[]{:S(2)}) copy-start(bf16[2,1,1,1024,1024]{4,3,2,1,0:T(8,128)(2,1)} %param.11) | copy-start | bytes 12582916
  154.6 1.0 copy-start.5

commit v3 on v0

v3 whole, which is shorter than its diff:
```python
import functools

import jax
import jax.numpy as jnp
from jax import lax
from jax.experimental import pallas as pl
from jax.experimental.pallas import tpu as pltpu
from jax.sharding import Mesh
from jax.sharding import PartitionSpec as P


SWEEPS = 2
SIDE = 4
CAP = 4
TILE = 256
SX = ("sx_0", "sx_1")
SX_SY = ("sx_0", "sx_1", "sy")
LOW, HIGH = (0, 1), (3, 2)


def cost(flops, bytes_accessed):
    return pl.CostEstimate(flops=flops, bytes_accessed=bytes_accessed, transcendentals=0)


def room(mebibytes):
    return pltpu.CompilerParams(vmem_limit_bytes=mebibytes << 20)


def fill_slots(owner_ref, slots, used):
    children = owner_ref.shape[0]
    for o in range(SIDE * SIDE):
        used[o] = 0
    for s in range(SIDE * SIDE * CAP):
        slots[s] = children

    def put(c, carry):
        o = owner_ref[c]
        k = used[o]
        slots[o * CAP + k] = c
        used[o] = k + 1
        return carry

    lax.fori_loop(0, children, put, 0)


def owner_at(table_ref, f, ahead, beside):
    offsets = (ahead, beside) if f == 0 else (beside, ahead)
    row = lax.rem(table_ref[0] + offsets[0], SIDE)
    column = lax.rem(table_ref[1] + offsets[1], SIDE)
    return row * SIDE + column


def multiply(weights, stacked, out, at):
    rhs_count = out.shape[1]
    turned = weights[...].T
    for s in range(0, stacked.shape[1], TILE):
        product = jnp.dot(turned, stacked[:, s : s + TILE], preferred_element_type=jnp.float32)
        for b in range(2):
            piece = product[b * rhs_count : (b + 1) * rhs_count]
            out[at + b, :, s : s + TILE] = piece.astype(out.dtype)


def put_weights(weights, coeff_ref, f, c, filled, b, k):
    rank, rhs_count = coeff_ref.shape[2:]
    at = (b * CAP + k) * rank
    coeff = coeff_ref[f, c]
    weights[at : at + rank, b * rhs_count : (b + 1) * rhs_count] = jnp.where(
        filled, coeff, jnp.zeros_like(coeff)
    )


def owner_products(plan, shapes, owners, place, basis, coeff, after=(), fetched=False):
    _, children, rank, sep_size = basis.shape
    rhs_count = coeff.shape[3]
    count = len(plan) if fetched else 1
    depth = 2 * CAP * rank

    def body(owner_ref, table_ref, basis_ref, coeff_ref, *rest):
        outs = rest[len(after) : len(after) + len(shapes)]
        slots, used, stacked, weights = rest[len(after) + len(shapes) :][:4]
        arrived = rest[-1]
        fill_slots(owner_ref, slots, used)

        def child(f, ahead, beside, k):
            c = slots[owner_at(table_ref, f, ahead, beside) * CAP + k]
            filled = c < children
            return jnp.where(filled, c, 0), filled

        def copies(n):
            _, _, f, ahead, pair = plan[n]
            return [
                pltpu.make_async_copy(
                    basis_ref.at[f, child(f, ahead, beside, k)[0]],
                    stacked.at[n, pl.ds((b * CAP + k) * rank, rank)],
                    arrived.at[n],
                )
                for b, beside in enumerate(pair)
                for k in range(CAP)
            ]

        if fetched:
            flights = [copies(n) for n in range(len(plan))]
            for flight in flights:
                for copy in flight:
                    copy.start()
        weights[...] = jnp.zeros_like(weights)
        for n, (out, at, f, ahead, pair) in enumerate(plan):
            for b, beside in enumerate(pair):
                for k in range(CAP):
                    c, filled = child(f, ahead, beside, k)
                    put_weights(weights, coeff_ref, f, c, filled, b, k)
                    if not fetched:
                        stacked[0, pl.ds((b * CAP + k) * rank, rank)] = basis_ref[f, c]
            if fetched:
                for copy in flights[n]:
                    copy.wait()
            multiply(weights, stacked.at[n if fetched else 0], outs[out], at)

    space = pltpu.MemorySpace.HBM if fetched else pltpu.MemorySpace.VMEM
    return pl.pallas_call(
        body,
        in_specs=[pl.BlockSpec(memory_space=pltpu.MemorySpace.SMEM)] * 2
        + [pl.BlockSpec(memory_space=space), pl.BlockSpec(memory_space=pltpu.MemorySpace.VMEM)]
        + [pl.BlockSpec(memory_space=pl.ANY) for _ in after],
        out_specs=[pl.BlockSpec(memory_space=pltpu.MemorySpace.VMEM) for _ in shapes],
        scratch_shapes=[
            pltpu.SMEM((SIDE * SIDE * CAP,), jnp.int32),
            pltpu.SMEM((SIDE * SIDE,), jnp.int32),
            pltpu.VMEM((count, depth, sep_size), jnp.bfloat16),
            pltpu.VMEM((depth, 2 * rhs_count), jnp.bfloat16),
            pltpu.SemaphoreType.DMA((count,)),
        ],
        out_shape=[jax.ShapeDtypeStruct((n, rhs_count, sep_size), dtype) for n, dtype in shapes],
        compiler_params=room(57 if fetched else 16),
        cost_estimate=cost(
            2 * len(plan) * 4 * CAP * rank * sep_size * rhs_count * 2,
            len(plan) * 2 * (CAP * rank * sep_size * 2 + rhs_count * sep_size * 4),
        ),
    )(owners, place, basis, coeff, *after)


def in_vmem(count):
    return [pl.BlockSpec(memory_space=pltpu.MemorySpace.VMEM)] * count


def join(mine, got, whole):
    def body(mine_ref, got_ref, whole_ref, out_ref):
        n = mine_ref.shape[0]
        out_ref[:n] = (mine_ref[...] + got_ref[...].astype(jnp.float32)).astype(out_ref.dtype)

    return pl.pallas_call(
        body,
        in_specs=in_vmem(3),
        out_specs=in_vmem(1)[0],
        out_shape=jax.ShapeDtypeStruct(whole.shape, whole.dtype),
        input_output_aliases={2: 0},
        compiler_params=room(4),
        cost_estimate=cost(mine.size * 2, mine.size * 8),
    )(mine, got, whole)


def row_totals(own, low, high):
    _, rhs_count, sep_size = own.shape

    def body(own_ref, low_ref, high_ref, *outs):
        for at, out in enumerate(outs):
            crossed = (at + 2) % SIDE
            total = own_ref[at] + low_ref[at].astype(jnp.float32) + high_ref[crossed].astype(jnp.float32)
            out[...] = total.astype(out.dtype)

    types = (jnp.float32,) * 3 + (jnp.bfloat16,)
    return pl.pallas_call(
        body,
        in_specs=in_vmem(3),
        out_specs=in_vmem(SIDE),
        out_shape=[jax.ShapeDtypeStruct((rhs_count, sep_size), dtype) for dtype in types],
        compiler_params=room(4),
        cost_estimate=cost(own.size * 2, own.size * 12),
    )(own, low, high)


def across(field, matrix_tile):
    return lax.dot_general(
        field, matrix_tile, (((1,), (1,)), ((), ())), preferred_element_type=jnp.float32
    )


def staged(sep_rhs, matrix):
    f_local, sep_size, rhs_count = sep_rhs.shape

    def body(rhs_ref, matrix_ref, out_ref, held_ref):
        for f in range(f_local):
            for s in range(0, sep_size, TILE):
                out_ref[f, :, s : s + TILE] = rhs_ref[f, s : s + TILE, :].astype(jnp.float32).T
                held_ref[f, s : s + TILE] = matrix_ref[f, s : s + TILE]

    return pl.pallas_call(
        body,
        in_specs=in_vmem(2),
        out_specs=in_vmem(2),
        out_shape=[
            jax.ShapeDtypeStruct((f_local, rhs_count, sep_size), jnp.float32),
            jax.ShapeDtypeStruct(matrix.shape, matrix.dtype),
        ],
        compiler_params=room(4),
        cost_estimate=cost(sep_rhs.size, sep_rhs.size * 6 + matrix.size * 4),
    )(sep_rhs, matrix)


def first_solve(rhs, parts, matrix):
    f_local, rhs_count, sep_size = rhs.shape

    def body(rhs_ref, *rest):
        parts_refs, (matrix_ref, right_ref, out_ref, sent_ref) = rest[:-4], rest[-4:]
        for f in range(f_local):
            right = rhs_ref[f]
            for part in parts_refs[SIDE * f : SIDE * f + SIDE]:
                right = right - part[...].astype(jnp.float32)
            right_ref[f] = right
            field = right.astype(jnp.bfloat16)
            for s in range(0, sep_size, TILE):
                out = across(field, matrix_ref[f, s : s + TILE])
                out_ref[f, :, s : s + TILE] = out
                sent_ref[f, :, s : s + TILE] = out.astype(jnp.bfloat16)

    return pl.pallas_call(
        body,
        in_specs=in_vmem(2 + len(parts)),
        out_specs=in_vmem(3),
        out_shape=[jax.ShapeDtypeStruct(rhs.shape, t) for t in (jnp.float32, jnp.float32, jnp.bfloat16)],
        compiler_params=room(8),
        cost_estimate=cost(2 * matrix.size * rhs_count, matrix.size * 2 + rhs.size * 24),
    )(rhs, *parts, matrix)


def residual_of(f, table_ref, right_ref, mine_ref, around_refs, coupling_ref):
    residual = right_ref[f] - mine_ref[f]
    for n, around in enumerate(around_refs):
        coupled = coupling_ref[f, pl.ds(table_ref[2 + n], 1), :]
        residual = residual + coupled * around[f].astype(jnp.float32)
    return residual


def sweep(table, right_side, mine, around, coupling, matrix):
    f_local, rhs_count, sep_size = mine.shape

    def body(table_ref, right_ref, mine_ref, *rest):
        around_refs, (coupling_ref, matrix_ref, out_ref, sent_ref) = rest[:4], rest[4:]
        for f in range(f_local):
            residual = residual_of(f, table_ref, right_ref, mine_ref, around_refs, coupling_ref)
            field = residual.astype(jnp.bfloat16)
            for s in range(0, sep_size, TILE):
                out = mine_ref[f, :, s : s + TILE] + across(field, matrix_ref[f, s : s + TILE])
                out_ref[f, :, s : s + TILE] = out
                sent_ref[f, :, s : s + TILE] = out.astype(jnp.bfloat16)

    return pl.pallas_call(
        body,
        in_specs=[pl.BlockSpec(memory_space=pltpu.MemorySpace.SMEM)] + in_vmem(8),
        out_specs=in_vmem(2),
        out_shape=[jax.ShapeDtypeStruct(mine.shape, t) for t in (jnp.float32, jnp.bfloat16)],
        compiler_params=room(8),
        cost_estimate=cost(2 * matrix.size * rhs_count, matrix.size * 2 + mine.size * 24),
    )(table, right_side, mine, *around, coupling, matrix)


def last_sweep(table, right_side, mine, around, coupling, matrix, copies):
    f_local, rhs_count, sep_size = mine.shape

    def body(table_ref, right_ref, mine_ref, *rest):
        around_refs, (coupling_ref, matrix_ref, out_ref, sum_ref) = rest[:4], rest[4:]
        total = 0.0
        for f in range(f_local):
            residual = residual_of(f, table_ref, right_ref, mine_ref, around_refs, coupling_ref)
            field = residual.astype(jnp.bfloat16)
            square = jnp.sum(residual * residual, axis=0, keepdims=True)
            total = total + square * table_ref[6 + f].astype(jnp.float32)
            for s in range(0, sep_size, TILE):
                step = across(matrix_ref[f, s : s + TILE], field)
                out_ref[f, s : s + TILE, :] = mine_ref[f, :, s : s + TILE].T + step
        sum_ref[...] = jnp.broadcast_to(jnp.sum(total), sum_ref.shape)

    return pl.pallas_call(
        body,
        in_specs=[pl.BlockSpec(memory_space=pltpu.MemorySpace.SMEM)] + in_vmem(8),
        out_specs=in_vmem(2),
        out_shape=[
            jax.ShapeDtypeStruct((f_local, sep_size, rhs_count), jnp.float32),
            jax.ShapeDtypeStruct((copies, 8, 128), jnp.float32),
        ],
        compiler_params=room(8),
        cost_estimate=cost(2 * matrix.size * rhs_count, matrix.size * 2 + mine.size * 24),
    )(table, right_side, mine, *around, coupling, matrix)


def turn(x, axis, by):
    return lax.ppermute(x, axis, [(i, (i + by) % SIDE) for i in range(SIDE)])


def neighbours(x, axis, count):
    pairs = [[(i, i + 1) for i in range(first, count - 1, 2)] for first in range(2)]
    return tuple(lax.ppermute(x, axis, p + [(b, a) for a, b in p]) for p in pairs)


def on_device(update_basis, update_coeff, owner, sep_rhs, coupling, frontal_inverse):
    f_local = update_basis.shape[0]
    sep_size = update_basis.shape[3]
    rhs_count = update_coeff.shape[3]
    columns, rows = lax.axis_size(SX), lax.axis_size("sy")
    odd = [lax.rem(lax.axis_index(axis).astype(jnp.int32), 2) for axis in (SX, "sy")]
    freq_ids = [lax.axis_index("freq").astype(jnp.int32) * f_local + f + 1 for f in range(f_local)]
    place = [lax.axis_index(axis).astype(jnp.int32) for axis in SX]
    rows_of = [1 - odd[0], odd[0], 3 - odd[1], 2 + odd[1]]
    table = jnp.stack(place + rows_of + [i * i for i in freq_ids])
    data = (owner[:, 0], table, update_basis, update_coeff)
    half, full = jnp.bfloat16, jnp.float32

    axes = (SX, SX[::-1])
    plan = tuple((2 * f + n, 0, f, 2, pair) for f in range(2) for n, pair in enumerate((LOW, HIGH)))
    far = owner_products(plan, ((2, half),) * 4, *data, fetched=True)
    got = [(turn(far[2 * f], axes[f][0], 1), turn(far[2 * f + 1], axes[f][0], -1)) for f in range(2)]

    sides = ((1, LOW, HIGH), (3, HIGH, LOW))
    plan = tuple(
        (4 * late + 2 * f + n, 2 * late, f, ahead, pairs[late])
        for f in range(2)
        for n, (ahead, *pairs) in enumerate(sides)
        for late in range(2)
    )
    near = owner_products(plan, ((2, full),) * 4 + ((4, half),) * 4, *data)

    sums, joined = [], []
    for f in range(2):
        following = join(near[2 * f], got[f][0], near[4 + 2 * f])
        preceding = join(near[2 * f + 1], got[f][1], near[5 + 2 * f])
        joined += [following, preceding]
        sums.append((turn(following, axes[f][0], 1), turn(preceding, axes[f][0], -1)))
    plan = tuple((f, 2 * n, f, 0, pair) for f in range(2) for n, pair in enumerate((LOW, HIGH)))
    own = owner_products(plan, ((4, full),) * 2, *data, after=tuple(joined))
    rhs, matrix = staged(sep_rhs[:, 0, 0], frontal_inverse[:, 0, 0])

    parts = []
    for f in range(2):
        here, following, preceding, opposite = row_totals(own[f], *sums[f])
        axis = axes[f][1]
        parts += [here, turn(opposite, axis, 2), turn(following, axis, 1), turn(preceding, axis, -1)]

    coupling_rows = coupling[:, 0, 0]
    right_side, mine, sent = first_solve(rhs, parts, matrix)
    for _ in range(SWEEPS - 1):
        around = neighbours(sent, SX, columns) + neighbours(sent, "sy", rows)
        mine, sent = sweep(table, right_side, mine, around, coupling_rows, matrix)
    around = neighbours(sent, SX, columns) + neighbours(sent, "sy", rows)
    group = ("sy", "freq")
    solution, squares = last_sweep(
        table, right_side, mine, around, coupling_rows, matrix, lax.axis_size(group)
    )
    squares = jnp.sum(lax.all_to_all(squares, group, 0, 0, tiled=True), axis=0)
    squares = jnp.broadcast_to(squares, (columns, *squares.shape))
    squares = jnp.sum(lax.all_to_all(squares, SX, 0, 0, tiled=True), axis=0)
    entries = float(f_local * lax.axis_size("freq") * columns * rows * sep_size * rhs_count)
    residual_total = jnp.sqrt(squares[0, 0] / entries + 1e-06)
    return (solution[:, None, None], residual_total)


def solution(mesh):
    finer = Mesh(
        mesh.devices.reshape(SIDE, SIDE, mesh.shape["sy"], mesh.shape["freq"]),
        ("sx_0", "sx_1", "sy", "freq"),
    )
    return jax.shard_map(
        on_device,
        mesh=finer,
        in_specs=(
            P("freq", SX_SY, None, None),
            P("freq", SX_SY, None, None),
            P(SX_SY, None),
            P("freq", SX, "sy", None, None),
            P("freq", SX, "sy", None, None),
            P("freq", SX, "sy", None, None),
        ),
        out_specs=(P("freq", SX, "sy", None, None), P()),
        check_vma=False,
    )
```

time: 237 us -> 152 us (0.64)
  blocking collectives: 151 us -> 36.4 us
  waiting for transfers between devices: 15.2 us -> 56.1 us
  Pallas kernels: 0 us -> 18.3 us
  other arithmetic: 16.3 us -> 0.04 us
  matrix products: 11.3 us -> 0 us
  local copies, waits for them, and re-layouts: 8.41 us -> 1.19 us
  starting transfers between devices: 31.5 us -> 37 us
    all_to_all x1 -> x2, blocking collectives: 101 us -> 36.4 us  [the longest x1 23.9 us: on_device(): squares = jnp.sum(lax.all_to_all(squares, group, 0, 0, tiled=True), axis=0)]
    psum x4 -> x0, blocking collectives: 50 us -> none  [by_axis(): return functools.reduce(lax.psum, axes, x)]
    ppermute x8 -> x22, waiting for transfers between devices: 14.2 us -> 56.1 us  [the longest x14 40.5 us: turn(): return lax.ppermute(x, axis, [(i, (i + by) % SIDE) for i in range(SIDE)])]
    pallas_call x0 -> x13, Pallas kernels: none -> 18.3 us  [the longest x3 9.65 us: owner_products(): pl.pallas_call(body, in_specs=[pl.BlockSpec(memory_space=pltpu.MemorySpac...]
    ppermute x8 -> x22, starting transfers between devices: 23.9 us -> 37 us  [the longest x14 21.4 us: turn(): return lax.ppermute(x, axis, [(i, (i + by) % SIDE) for i in range(SIDE)])]
    dot_general x4 -> x0, matrix products: 11.3 us -> none  [the longest x3 7.77 us: apply_inverse(): jnp.einsum('fst,ftn->fsn', inverse_block, field.astype(jnp.bfloat16), pre...]
    select_n x3 -> x0, other arithmetic: 8.67 us -> none  [the longest x2 7.48 us: on_device(): basis_slots = jnp.take(update_basis, source_child, axis=1)]
    gather x2 -> x0, local copies, waits for them, and re-layouts: 8.35 us -> none  [the longest x1 7.6 us: on_device(): basis_slots = jnp.take(update_basis, source_child, axis=1)]
  transfers between devices with their start and end apart: 9 -> 22, of which waited for: 7 -> 9; matrix products, arithmetic and copies ran while one was open for 6% -> 0% of each run, Pallas kernels for 0% -> 4%
where the time goes in v3:
time: 152 us
  waiting for transfers between devices  56.1 us (37%)
  starting transfers between devices  37 us (24%)
  blocking collectives  36.4 us (24%)
  Pallas kernels  18.3 us (12%)
  between operations  2.68 us (2%)
    ppermute x14, waiting for transfers between devices, turn(): return lax.ppermute(x, axis, [(i, (i + by) % SIDE) for i in range(SIDE)])  40.5 us
    all_to_all x1, blocking collectives, on_device(): squares = jnp.sum(lax.all_to_all(squares, group, 0, 0, tiled=True), axis=0)  23.9 us
    ppermute x14, starting transfers between devices, turn(): return lax.ppermute(x, axis, [(i, (i + by) % SIDE) for i in range(SIDE)])  21.4 us
    ppermute x8, starting transfers between devices, neighbours(): lax.ppermute(x, axis, p + [(b, a) for a, b in p])  15.6 us
    ppermute x8, waiting for transfers between devices, neighbours(): lax.ppermute(x, axis, p + [(b, a) for a, b in p])  15.5 us
    all_to_all x1, blocking collectives, on_device(): squares = jnp.sum(lax.all_to_all(squares, SX, 0, 0, tiled=True), axis=0)  12.5 us
    pallas_call x3, Pallas kernels, owner_products(): pl.pallas_call(body, in_specs=[pl.BlockSpec(memory_space=pltpu.MemorySpac...  9.65 us
    pallas_call x1, Pallas kernels, last_sweep(): pl.pallas_call(body, in_specs=[pl.BlockSpec(memory_space=pltpu.MemorySpac...  3.5 us
  transfers between devices with their start and end apart: 22, of which 9 were waited for; matrix products, arithmetic and copies ran while one was open for 0% of the time, Pallas kernels for 4%

profile of v3, /device:TPU:1, one launch (start us, length us, event | category | flops | bytes accessed | tf_op | source)
XLA Modules:
  0.0 151.7 jit_solution(18163819753811313917)
XLA Ops:
  0.6 0.0 copy-start.6
  0.7 0.6 stack.35.table_ref
  1.3 5.4 %shard_map.79 = (bf16[2,128,1024]{2,1,0:T(8,128)(2,1)}, bf16[2,128,1024]{2,1,0:T(8,128)(2,1)}, bf16[2,128,1024]{2,1,0:T(8,128)(2,1)}, bf16[2,128,1024]{2,1,0:T(8,128)(2,1)}) custom-call(s32[32]{0:T(128)} %bitcast.20, s32[8]{0:T(128)} %stack.35.table_ref, bf16[2,32,32,1024]{3,2,1,0:T(8,128)(2,1)} %basis_ref.5, bf16[2,32,32,128]{3,2,1,0:T(8,128)(2,1)} %coeff_ref.5), custom_call_target="tpu_custom_call" | custom-call | flops 1073741824 | bytes 6291456 | tf_op jit(solution)/shard_map/pallas_call | solution.py:120
  6.7 3.4 %collective-permute-start.3 = (bf16[2,128,1024]{2,1,0:T(8,128)(2,1)}, bf16[2,128,1024]{2,1,0:T(8,128)(2,1)S(1)}, u32[]{:S(2)}, u32[]{:S(2)}) collective-permute-start(bf16[2,128,1024]{2,1,0:T(8,128)(2,1)} %get-tuple-element.44), channel_id=1, source_target_pairs={{0,48},{16,0},{32,16},{48,32},{1,49},{17,1},{33,17},{49,33},{2,50}... | collective-permute-start | bytes 1572872 | tf_op jit(solution)/shard_map/ppermute | solution.py:297
  10.1 2.6 %collective-permute-start.1 = (bf16[2,128,1024]{2,1,0:T(8,128)(2,1)}, bf16[2,128,1024]{2,1,0:T(8,128)(2,1)S(1)}, u32[]{:S(2)}, u32[]{:S(2)}) collective-permute-start(bf16[2,128,1024]{2,1,0:T(8,128)(2,1)} %get-tuple-element.38), channel_id=1, source_target_pairs={{0,192},{64,0},{128,64},{192,128},{1,193},{65,1},{129,65},{193,129... | collective-permute-start | bytes 1572872 | tf_op jit(solution)/shard_map/ppermute | solution.py:297
  12.8 2.4 %shard_map.78 = (f32[2,128,1024]{2,1,0:T(8,128)S(1)}, f32[2,128,1024]{2,1,0:T(8,128)S(1)}, f32[2,128,1024]{2,1,0:T(8,128)S(1)}, f32[2,128,1024]{2,1,0:T(8,128)S(...) custom-call(s32[32]{0:T(128)S(1)} %bitcast.21, ...), custom_call_target="tpu_custom_call" | custom-call | flops 2147483648 | bytes 12582912 | tf_op jit(solution)/shard_map/pallas_call | solution.py:120
  15.2 5.9 %collective-permute-done.3.got_ref = bf16[2,128,1024]{2,1,0:T(8,128)(2,1)S(1)} collective-permute-done((bf16[2,128,1024]{2,1,0:T(8,128)(2,1)}, bf16[2,128,1024]{2,1,0:T(8,128)(2,1)S(1)}, u32[]{:S(2)}, u32[]{:S(2)}) %collective-permute-start.3) | collective-permute-done | bytes 524320 | tf_op jit(solution)/shard_map/ppermute | solution.py:297
  21.0 0.1 shard_map.83.rest_3_
  21.1 3.4 %collective-permute-start.10 = (bf16[4,128,1024]{2,1,0:T(8,128)(2,1)S(1)}, bf16[4,128,1024]{2,1,0:T(8,128)(2,1)S(1)}, u32[]{:S(2)}, u32[]{:S(2)}) collective-permute-start(bf16[4,128,1024]{2,1,0:T(8,128)(2,1)S(1)} %shard_map.83.rest_3_), channel_id=1, source_target_pairs={{0,48},{16,0},{32,16},{48,32},{1,49},{17,1},{33,17},{49,33},{2,50}... | collective-permute-start | bytes 3145736 | tf_op jit(solution)/shard_map/ppermute | solution.py:297
  24.5 0.1 shard_map.82.rest_2_
  24.6 0.1 collective-permute-start.9
  24.7 0.1 shard_map.81.rest_1_
  24.8 2.7 %collective-permute-start.5 = (bf16[4,128,1024]{2,1,0:T(8,128)(2,1)S(1)}, bf16[4,128,1024]{2,1,0:T(8,128)(2,1)S(1)}, u32[]{:S(2)}, u32[]{:S(2)}) collective-permute-start(bf16[4,128,1024]{2,1,0:T(8,128)(2,1)S(1)} %shard_map.81.rest_1_), channel_id=1, source_target_pairs={{0,192},{64,0},{128,64},{192,128},{1,193},{65,1},{129,65},{193,129... | collective-permute-start | bytes 3145736 | tf_op jit(solution)/shard_map/ppermute | solution.py:297
  27.5 0.1 shard_map.80.rest_0_
  27.6 0.1 collective-permute-start.4
  27.7 1.8 %shard_map.84 = (f32[4,128,1024]{2,1,0:T(8,128)S(1)}, f32[4,128,1024]{2,1,0:T(8,128)S(1)}) custom-call(s32[32]{0:T(128)S(1)} %bitcast.22, s32[8]{0:T(128)S(1)} %copy-done.5, bf16[2,32,32,1024]{3,2,1,0:T(8,128)(2,1)S(1)} %copy-done, bf16[2,32,32,128]{3,2,1,0:T(8,128)(2,1)S(1)} %copy-done.2, bf16[4,128,1024]{2,1,0:T(8,128)(2,1)S(1)} %shard_map.80.rest_0_, ...), custom_call_target="tpu_custom_call" | custom-call | flops 1073741824 | bytes 6291456 | tf_op jit(solution)/shard_map/pallas_call | solution.py:120
  29.5 16.0 %collective-permute-done.10.high_ref = bf16[4,128,1024]{2,1,0:T(8,128)(2,1)S(1)} collective-permute-done((bf16[4,128,1024]{2,1,0:T(8,128)(2,1)S(1)}, bf16[4,128,1024]{2,1,0:T(8,128)(2,1)S(1)}, u32[]{:S(2)}, u32[]{:S(2)}) %collective-permute-start.10) | collective-permute-done | bytes 1048608 | tf_op jit(solution)/shard_map/ppermute | solution.py:297
  45.5 3.3 %collective-permute-done.9.low_ref = bf16[4,128,1024]{2,1,0:T(8,128)(2,1)S(1)} collective-permute-done((bf16[4,128,1024]{2,1,0:T(8,128)(2,1)S(1)}, bf16[4,128,1024]{2,1,0:T(8,128)(2,1)S(1)}, u32[]{:S(2)}, u32[]{:S(2)}) %collective-permute-start.9) | collective-permute-done | bytes 1048608 | tf_op jit(solution)/shard_map/ppermute | solution.py:297
  48.8 0.3 shard_map.86
  49.1 1.4 collective-permute-start.12
  50.5 1.4 collective-permute-start.13
  51.9 1.6 %collective-permute-start.11 = (bf16[128,1024]{1,0:T(8,128)(2,1)S(1)}, bf16[128,1024]{1,0:T(8,128)(2,1)S(1)}, u32[]{:S(2)}, u32[]{:S(2)}) collective-permute-start(bf16[128,1024]{1,0:T(8,128)(2,1)S(1)} %get-tuple-element.53), channel_id=1, source_target_pairs={{0,128},{64,192},{128,0},{192,64},{1,129},{65,193},{129,1},{193,65... | collective-permute-start | bytes 786440 | tf_op jit(solution)/shard_map/ppermute | solution.py:297
  53.5 0.3 shard_map.85
  53.8 0.1 collective-permute-start.7
  53.8 2.7 %collective-permute-start.8 = (f32[128,1024]{1,0:T(8,128)S(1)}, f32[128,1024]{1,0:T(8,128)S(1)}, u32[]{:S(2)}, u32[]{:S(2)}) collective-permute-start(f32[128,1024]{1,0:T(8,128)S(1)} %get-tuple-element.50), channel_id=1, source_target_pairs={{0,48},{16,0},{32,16},{48,32},{1,49},{17,1},{33,17},{49,33},{2,50}... | collective-permute-start | bytes 1572872 | tf_op jit(solution)/shard_map/ppermute | solution.py:297
  56.5 11.1 %collective-permute-done.11.rest_5_ = bf16[128,1024]{1,0:T(8,128)(2,1)S(1)} collective-permute-done((bf16[128,1024]{1,0:T(8,128)(2,1)S(1)}, bf16[128,1024]{1,0:T(8,128)(2,1)S(1)}, u32[]{:S(2)}, u32[]{:S(2)}) %collective-permute-start.11) | collective-permute-done | bytes 262176 | tf_op jit(solution)/shard_map/ppermute | solution.py:297
  67.6 2.1 %collective-permute-start.6 = (bf16[128,1024]{1,0:T(8,128)(2,1)S(1)}, bf16[128,1024]{1,0:T(8,128)(2,1)S(1)}, u32[]{:S(2)}, u32[]{:S(2)}) collective-permute-start(bf16[128,1024]{1,0:T(8,128)(2,1)S(1)} %get-tuple-element.48), channel_id=1, source_target_pairs={{0,32},{16,48},{32,0},{48,16},{1,33},{17,49},{33,1},{49,17},{2,34}... | collective-permute-start | bytes 786440 | tf_op jit(solution)/shard_map/ppermute | solution.py:297
  69.7 0.4 shard_map.77
  70.1 4.2 %collective-permute-done.6.rest_1_ = bf16[128,1024]{1,0:T(8,128)(2,1)S(1)} collective-permute-done((bf16[128,1024]{1,0:T(8,128)(2,1)S(1)}, bf16[128,1024]{1,0:T(8,128)(2,1)S(1)}, u32[]{:S(2)}, u32[]{:S(2)}) %collective-permute-start.6) | collective-permute-done | bytes 262176 | tf_op jit(solution)/shard_map/ppermute | solution.py:297
  74.4 0.0 copy-start.4
  74.4 1.6 %shard_map.87 = (f32[2,128,1024]{2,1,0:T(8,128)S(1)}, f32[2,128,1024]{2,1,0:T(8,128)S(1)}, bf16[2,128,1024]{2,1,0:T(8,128)(2,1)S(1)}) custom-call(f32[2,128,1024]{2,1,0:T(8,128)S(1)} %get-tuple-element.33.rhs_ref, f32[128,1024]{1,0:T(8,128)S(1)} %get-tuple-element.47.rest_0_, bf16[128,1024]{1,0:T(8,128)(2,1)S(1)} %collective-permute-done.6.rest_1_, ...), custom_call_target="tpu_custom_call" | custom-call | flops 536870912 | bytes 10485760 | tf_op jit(solution)/shard_map/pallas_call | solution.py:226
  76.0 2.0 %collective-permute-start.14 = (bf16[2,128,1024]{2,1,0:T(8,128)(2,1)S(1)}, bf16[2,128,1024]{2,1,0:T(8,128)(2,1)S(1)}, u32[]{:S(2)}, u32[]{:S(2)}) collective-permute-start(bf16[2,128,1024]{2,1,0:T(8,128)(2,1)S(1)} %get-tuple-element.59), channel_id=1, source_target_pairs={{0,16},{32,48},{64,80},{96,112},{128,144},{160,176},{192,208},{224... | collective-permute-start | bytes 1572872 | tf_op jit(solution)/shard_map/ppermute | solution.py:302
  78.0 0.7 collective-permute-start.15
  78.7 1.7 %collective-permute-start.16 = (bf16[2,128,1024]{2,1,0:T(8,128)(2,1)S(1)}, bf16[2,128,1024]{2,1,0:T(8,128)(2,1)S(1)}, u32[]{:S(2)}, u32[]{:S(2)}) collective-permute-start(bf16[2,128,1024]{2,1,0:T(8,128)(2,1)S(1)} %get-tuple-element.59), channel_id=1, source_target_pairs={{0,2},{4,6},{8,10},{12,14},{2,0},{6,4},{10,8},{14,12},{1,3},{5,7},... | collective-permute-start | bytes 1572872 | tf_op jit(solution)/shard_map/ppermute | solution.py:302
  80.4 0.7 collective-permute-start.17
  81.1 5.4 %collective-permute-done.14.rest_0_ = bf16[2,128,1024]{2,1,0:T(8,128)(2,1)S(1)} collective-permute-done((bf16[2,128,1024]{2,1,0:T(8,128)(2,1)S(1)}, bf16[2,128,1024]{2,1,0:T(8,128)(2,1)S(1)}, u32[]{:S(2)}, u32[]{:S(2)}) %collective-permute-start.14) | collective-permute-done | bytes 524320 | tf_op jit(solution)/shard_map/ppermute | solution.py:302
  86.5 3.1 %collective-permute-done.16.rest_2_ = bf16[2,128,1024]{2,1,0:T(8,128)(2,1)S(1)} collective-permute-done((bf16[2,128,1024]{2,1,0:T(8,128)(2,1)S(1)}, bf16[2,128,1024]{2,1,0:T(8,128)(2,1)S(1)}, u32[]{:S(2)}, u32[]{:S(2)}) %collective-permute-start.16) | collective-permute-done | bytes 524320 | tf_op jit(solution)/shard_map/ppermute | solution.py:302
  89.6 2.2 %shard_map.88 = (f32[2,128,1024]{2,1,0:T(8,128)S(1)}, bf16[2,128,1024]{2,1,0:T(8,128)(2,1)S(1)}) custom-call(s32[8]{0:T(128)S(1)} %copy-done.5, f32[2,128,1024]{2,1,0:T(8,128)S(1)} %get-tuple-element.57.right_ref, f32[2,128,1024]{2,1,0:T(8,128)S(1)} %get-tuple-element.58.mine_ref, bf16[2,128,1024]{2,1,0:T(8,128)(2,1)S(1)} %collective-permute-done.14.rest_0_, ...), custom_call_target="tpu_custom_call" | custom-call | flops 536870912 | bytes 10485760 | tf_op jit(solution)/shard_map/pallas_call | solution.py:257
  91.7 4.2 %collective-permute-start.18 = (bf16[2,128,1024]{2,1,0:T(8,128)(2,1)S(1)}, bf16[2,128,1024]{2,1,0:T(8,128)(2,1)S(1)}, u32[]{:S(2)}, u32[]{:S(2)}) collective-permute-start(bf16[2,128,1024]{2,1,0:T(8,128)(2,1)S(1)} %get-tuple-element.61), channel_id=1, source_target_pairs={{0,16},{32,48},{64,80},{96,112},{128,144},{160,176},{192,208},{224... | collective-permute-start | bytes 1572872 | tf_op jit(solution)/shard_map/ppermute | solution.py:302
  96.0 0.7 collective-permute-start.19
  96.7 4.9 %collective-permute-start.20 = (bf16[2,128,1024]{2,1,0:T(8,128)(2,1)S(1)}, bf16[2,128,1024]{2,1,0:T(8,128)(2,1)S(1)}, u32[]{:S(2)}, u32[]{:S(2)}) collective-permute-start(bf16[2,128,1024]{2,1,0:T(8,128)(2,1)S(1)} %get-tuple-element.61), channel_id=1, source_target_pairs={{0,2},{4,6},{8,10},{12,14},{2,0},{6,4},{10,8},{14,12},{1,3},{5,7},... | collective-permute-start | bytes 1572872 | tf_op jit(solution)/shard_map/ppermute | solution.py:302
  101.6 0.7 collective-permute-start.21
  102.3 2.0 %collective-permute-done.18.rest_0_ = bf16[2,128,1024]{2,1,0:T(8,128)(2,1)S(1)} collective-permute-done((bf16[2,128,1024]{2,1,0:T(8,128)(2,1)S(1)}, bf16[2,128,1024]{2,1,0:T(8,128)(2,1)S(1)}, u32[]{:S(2)}, u32[]{:S(2)}) %collective-permute-start.18) | collective-permute-done | bytes 524320 | tf_op jit(solution)/shard_map/ppermute | solution.py:302
  104.3 5.1 %collective-permute-done.20.rest_2_ = bf16[2,128,1024]{2,1,0:T(8,128)(2,1)S(1)} collective-permute-done((bf16[2,128,1024]{2,1,0:T(8,128)(2,1)S(1)}, bf16[2,128,1024]{2,1,0:T(8,128)(2,1)S(1)}, u32[]{:S(2)}, u32[]{:S(2)}) %collective-permute-start.20) | collective-permute-done | bytes 524320 | tf_op jit(solution)/shard_map/ppermute | solution.py:302
  109.4 3.5 %shard_map.89 = (f32[2,1024,128]{2,1,0:T(8,128)}, f32[16,8,128]{2,1,0:T(8,128)S(1)}) custom-call(s32[8]{0:T(128)S(1)} %copy-done.5, f32[2,128,1024]{2,1,0:T(8,128)S(1)} %get-tuple-element.57.right_ref, f32[2,128,1024]{2,1,0:T(8,128)S(1)} %get-tuple-element.60.mine_ref, bf16[2,128,1024]{2,1,0:T(8,128)(2,1)S(1)} %collective-permute-done.18.rest_0_, ...), custom_call_target="tpu_custom_call" | custom-call | flops 536870912 | bytes 10485760 | tf_op jit(solution)/shard_map/pallas_call | solution.py:283
  112.9 23.9 %all_to_all.10 = f32[16,8,128]{2,1,0:T(8,128)S(1)} all-to-all(f32[16,8,128]{2,1,0:T(8,128)S(1)} %get-tuple-element.63), channel_id=1, replica_groups=mesh['sx_0'=4,'sx_1'=4,'sy'=8,'freq'=2] {'sy','freq'}, dimensions={0} | all-to-all | bytes 131072 | tf_op jit(solution)/shard_map/all_to_all | solution.py:358
  136.8 12.5 %all_to_all.11 = f32[16,8,128]{2,1,0:T(8,128)S(1)} all-to-all(f32[16,8,128]{2,1,0:T(8,128)S(1)} %broadcast_in_dim.7), channel_id=1, replica_groups=mesh['sx_0'=4,'sx_1'=4,'sy'=8,'freq'=2] {'sx_0','sx_1'}, dimensions={0} | all-to-all | bytes 131072 | tf_op jit(solution)/shard_map/all_to_all | solution.py:360
  149.4 0.5 slice.3
  (30 shorter events, 0.1 us)
Async XLA Ops:
  0.6 12.1 %copy-start.6 = (s32[32,1]{0,1:T(1,128)S(1)}, s32[32,1]{0,1:T(1,128)}, u32[]{:S(2)}) copy-start(s32[32,1]{0,1:T(1,128)} %param.8) | copy-start | bytes 388
  0.6 12.1 %copy-start.2 = (bf16[2,32,32,128]{3,2,1,0:T(8,128)(2,1)S(1)}, bf16[2,32,32,128]{3,2,1,0:T(8,128)(2,1)}, u32[]{:S(2)}) copy-start(bf16[2,32,32,128]{3,2,1,0:T(8,128)(2,1)} %coeff_ref.5) | copy-start | bytes 1572868
  1.3 11.4 %copy-start = (bf16[2,32,32,1024]{3,2,1,0:T(8,128)(2,1)S(1)}, bf16[2,32,32,1024]{3,2,1,0:T(8,128)(2,1)}, u32[]{:S(2)}) copy-start(bf16[2,32,32,1024]{3,2,1,0:T(8,128)(2,1)} %basis_ref.5) | copy-start | bytes 12582916
  1.3 11.4 %copy-start.5 = (s32[8]{0:T(128)S(1)}, s32[8]{0:T(128)}, u32[]{:S(2)}) copy-start(s32[8]{0:T(128)} %stack.35.table_ref) | copy-start | bytes 100
  6.7 14.3 %collective-permute-start.3 = (bf16[2,128,1024]{2,1,0:T(8,128)(2,1)}, bf16[2,128,1024]{2,1,0:T(8,128)(2,1)S(1)}, u32[]{:S(2)}, u32[]{:S(2)}) collective-permute-start(bf16[2,128,1024]{2,1,0:T(8,128)(2,1)} %get-tuple-element.44), channel_id=1, source_target_pairs={{0,48},{16,0},{32,16},{48,32},{1,49},{17,1},{33,17},{49,33},{2,50}... | collective-permute-start | bytes 1572872 | tf_op jit(solution)/shard_map/ppermute | solution.py:297
  10.1 14.4 %collective-permute-start.2 = (bf16[2,128,1024]{2,1,0:T(8,128)(2,1)}, bf16[2,128,1024]{2,1,0:T(8,128)(2,1)S(1)}, u32[]{:S(2)}, u32[]{:S(2)}) collective-permute-start(bf16[2,128,1024]{2,1,0:T(8,128)(2,1)} %get-tuple-element.41), channel_id=1, source_target_pairs={{0,16},{16,32},{32,48},{48,0},{1,17},{17,33},{33,49},{49,1},{2,18}... | collective-permute-start | bytes 1572872 | tf_op jit(solution)/shard_map/ppermute | solution.py:297
  10.1 14.6 %collective-permute-start.1 = (bf16[2,128,1024]{2,1,0:T(8,128)(2,1)}, bf16[2,128,1024]{2,1,0:T(8,128)(2,1)S(1)}, u32[]{:S(2)}, u32[]{:S(2)}) collective-permute-start(bf16[2,128,1024]{2,1,0:T(8,128)(2,1)} %get-tuple-element.38), channel_id=1, source_target_pairs={{0,192},{64,0},{128,64},{192,128},{1,193},{65,1},{129,65},{193,129... | collective-permute-start | bytes 1572872 | tf_op jit(solution)/shard_map/ppermute | solution.py:297
  12.7 14.8 %collective-permute-start = (bf16[2,128,1024]{2,1,0:T(8,128)(2,1)}, bf16[2,128,1024]{2,1,0:T(8,128)(2,1)S(1)}, u32[]{:S(2)}, u32[]{:S(2)}) collective-permute-start(bf16[2,128,1024]{2,1,0:T(8,128)(2,1)} %get-tuple-element.35), channel_id=1, source_target_pairs={{0,64},{64,128},{128,192},{192,0},{1,65},{65,129},{129,193},{193,1... | collective-permute-start | bytes 1572872 | tf_op jit(solution)/shard_map/ppermute | solution.py:297
  21.1 24.4 %collective-permute-start.10 = (bf16[4,128,1024]{2,1,0:T(8,128)(2,1)S(1)}, bf16[4,128,1024]{2,1,0:T(8,128)(2,1)S(1)}, u32[]{:S(2)}, u32[]{:S(2)}) collective-permute-start(bf16[4,128,1024]{2,1,0:T(8,128)(2,1)S(1)} %shard_map.83.rest_3_), channel_id=1, source_target_pairs={{0,48},{16,0},{32,16},{48,32},{1,49},{17,1},{33,17},{49,33},{2,50}... | collective-permute-start | bytes 3145736 | tf_op jit(solution)/shard_map/ppermute | solution.py:297
  24.6 24.2 %collective-permute-start.9 = (bf16[4,128,1024]{2,1,0:T(8,128)(2,1)S(1)}, bf16[4,128,1024]{2,1,0:T(8,128)(2,1)S(1)}, u32[]{:S(2)}, u32[]{:S(2)}) collective-permute-start(bf16[4,128,1024]{2,1,0:T(8,128)(2,1)S(1)} %shard_map.82.rest_2_), channel_id=1, source_target_pairs={{0,16},{16,32},{32,48},{48,0},{1,17},{17,33},{33,49},{49,1},{2,18}... | collective-permute-start | bytes 3145736 | tf_op jit(solution)/shard_map/ppermute | solution.py:297
  24.8 28.7 %collective-permute-start.5 = (bf16[4,128,1024]{2,1,0:T(8,128)(2,1)S(1)}, bf16[4,128,1024]{2,1,0:T(8,128)(2,1)S(1)}, u32[]{:S(2)}, u32[]{:S(2)}) collective-permute-start(bf16[4,128,1024]{2,1,0:T(8,128)(2,1)S(1)} %shard_map.81.rest_1_), channel_id=1, source_target_pairs={{0,192},{64,0},{128,64},{192,128},{1,193},{65,1},{129,65},{193,129... | collective-permute-start | bytes 3145736 | tf_op jit(solution)/shard_map/ppermute | solution.py:297
  27.6 25.9 %collective-permute-start.4 = (bf16[4,128,1024]{2,1,0:T(8,128)(2,1)S(1)}, bf16[4,128,1024]{2,1,0:T(8,128)(2,1)S(1)}, u32[]{:S(2)}, u32[]{:S(2)}) collective-permute-start(bf16[4,128,1024]{2,1,0:T(8,128)(2,1)S(1)} %shard_map.80.rest_0_), channel_id=1, source_target_pairs={{0,64},{64,128},{128,192},{192,0},{1,65},{65,129},{129,193},{193,1... | collective-permute-start | bytes 3145736 | tf_op jit(solution)/shard_map/ppermute | solution.py:297
  48.8 20.9 %copy-start.1 = (bf16[2,1,1,1024,1024]{4,3,2,1,0:T(8,128)(2,1)S(1)}, bf16[2,1,1,1024,1024]{4,3,2,1,0:T(8,128)(2,1)}, u32[]{:S(2)}) copy-start(bf16[2,1,1,1024,1024]{4,3,2,1,0:T(8,128)(2,1)} %param.11) | copy-start | bytes 12582916
  48.8 20.9 %copy-start.3 = (bf16[2,1,1,1024,128]{4,3,2,1,0:T(8,128)(2,1)S(1)}, bf16[2,1,1,1024,128]{4,3,2,1,0:T(8,128)(2,1)}, u32[]{:S(2)}) copy-start(bf16[2,1,1,1024,128]{4,3,2,1,0:T(8,128)(2,1)} %param.9) | copy-start | bytes 1572868
  49.1 25.3 %collective-permute-start.12 = (f32[128,1024]{1,0:T(8,128)S(1)}, f32[128,1024]{1,0:T(8,128)S(1)}, u32[]{:S(2)}, u32[]{:S(2)}) collective-permute-start(f32[128,1024]{1,0:T(8,128)S(1)} %get-tuple-element.54), channel_id=1, source_target_pairs={{0,64},{64,128},{128,192},{192,0},{1,65},{65,129},{129,193},{193,1... | collective-permute-start | bytes 1572872 | tf_op jit(solution)/shard_map/ppermute | solution.py:297
  50.5 23.9 %collective-permute-start.13 = (f32[128,1024]{1,0:T(8,128)S(1)}, f32[128,1024]{1,0:T(8,128)S(1)}, u32[]{:S(2)}, u32[]{:S(2)}) collective-permute-start(f32[128,1024]{1,0:T(8,128)S(1)} %get-tuple-element.55), channel_id=1, source_target_pairs={{0,192},{64,0},{128,64},{192,128},{1,193},{65,1},{129,65},{193,129... | collective-permute-start | bytes 1572872 | tf_op jit(solution)/shard_map/ppermute | solution.py:297
  51.9 15.8 %collective-permute-start.11 = (bf16[128,1024]{1,0:T(8,128)(2,1)S(1)}, bf16[128,1024]{1,0:T(8,128)(2,1)S(1)}, u32[]{:S(2)}, u32[]{:S(2)}) collective-permute-start(bf16[128,1024]{1,0:T(8,128)(2,1)S(1)} %get-tuple-element.53), channel_id=1, source_target_pairs={{0,128},{64,192},{128,0},{192,64},{1,129},{65,193},{129,1},{193,65... | collective-permute-start | bytes 786440 | tf_op jit(solution)/shard_map/ppermute | solution.py:297
  53.8 20.6 %collective-permute-start.7 = (f32[128,1024]{1,0:T(8,128)S(1)}, f32[128,1024]{1,0:T(8,128)S(1)}, u32[]{:S(2)}, u32[]{:S(2)}) collective-permute-start(f32[128,1024]{1,0:T(8,128)S(1)} %get-tuple-element.49), channel_id=1, source_target_pairs={{0,16},{16,32},{32,48},{48,0},{1,17},{17,33},{33,49},{49,1},{2,18}... | collective-permute-start | bytes 1572872 | tf_op jit(solution)/shard_map/ppermute | solution.py:297
  53.8 20.5 %collective-permute-start.8 = (f32[128,1024]{1,0:T(8,128)S(1)}, f32[128,1024]{1,0:T(8,128)S(1)}, u32[]{:S(2)}, u32[]{:S(2)}) collective-permute-start(f32[128,1024]{1,0:T(8,128)S(1)} %get-tuple-element.50), channel_id=1, source_target_pairs={{0,48},{16,0},{32,16},{48,32},{1,49},{17,1},{33,17},{49,33},{2,50}... | collective-permute-start | bytes 1572872 | tf_op jit(solution)/shard_map/ppermute | solution.py:297
  67.6 6.7 %collective-permute-start.6 = (bf16[128,1024]{1,0:T(8,128)(2,1)S(1)}, bf16[128,1024]{1,0:T(8,128)(2,1)S(1)}, u32[]{:S(2)}, u32[]{:S(2)}) collective-permute-start(bf16[128,1024]{1,0:T(8,128)(2,1)S(1)} %get-tuple-element.48), channel_id=1, source_target_pairs={{0,32},{16,48},{32,0},{48,16},{1,33},{17,49},{33,1},{49,17},{2,34}... | collective-permute-start | bytes 786440 | tf_op jit(solution)/shard_map/ppermute | solution.py:297
  74.4 15.2 %copy-start.4 = (f32[2,1,1,4,1024]{4,3,2,1,0:T(4,128)S(1)}, f32[2,1,1,4,1024]{4,3,2,1,0:T(4,128)}, u32[]{:S(2)}) copy-start(f32[2,1,1,4,1024]{4,3,2,1,0:T(4,128)} %param.10) | copy-start | bytes 98308
  76.0 10.5 %collective-permute-start.14 = (bf16[2,128,1024]{2,1,0:T(8,128)(2,1)S(1)}, bf16[2,128,1024]{2,1,0:T(8,128)(2,1)S(1)}, u32[]{:S(2)}, u32[]{:S(2)}) collective-permute-start(bf16[2,128,1024]{2,1,0:T(8,128)(2,1)S(1)} %get-tuple-element.59), channel_id=1, source_target_pairs={{0,16},{32,48},{64,80},{96,112},{128,144},{160,176},{192,208},{224... | collective-permute-start | bytes 1572872 | tf_op jit(solution)/shard_map/ppermute | solution.py:302
  78.0 8.5 %collective-permute-start.15 = (bf16[2,128,1024]{2,1,0:T(8,128)(2,1)S(1)}, bf16[2,128,1024]{2,1,0:T(8,128)(2,1)S(1)}, u32[]{:S(2)}, u32[]{:S(2)}) collective-permute-start(bf16[2,128,1024]{2,1,0:T(8,128)(2,1)S(1)} %get-tuple-element.59), channel_id=1, source_target_pairs={{16,32},{48,64},{80,96},{112,128},{144,160},{176,192},{208,224},{3... | collective-permute-start | bytes 1572872 | tf_op jit(solution)/shard_map/ppermute | solution.py:302
  78.7 10.9 %collective-permute-start.16 = (bf16[2,128,1024]{2,1,0:T(8,128)(2,1)S(1)}, bf16[2,128,1024]{2,1,0:T(8,128)(2,1)S(1)}, u32[]{:S(2)}, u32[]{:S(2)}) collective-permute-start(bf16[2,128,1024]{2,1,0:T(8,128)(2,1)S(1)} %get-tuple-element.59), channel_id=1, source_target_pairs={{0,2},{4,6},{8,10},{12,14},{2,0},{6,4},{10,8},{14,12},{1,3},{5,7},... | collective-permute-start | bytes 1572872 | tf_op jit(solution)/shard_map/ppermute | solution.py:302
  80.4 9.1 %collective-permute-start.17 = (bf16[2,128,1024]{2,1,0:T(8,128)(2,1)S(1)}, bf16[2,128,1024]{2,1,0:T(8,128)(2,1)S(1)}, u32[]{:S(2)}, u32[]{:S(2)}) collective-permute-start(bf16[2,128,1024]{2,1,0:T(8,128)(2,1)S(1)} %get-tuple-element.59), channel_id=1, source_target_pairs={{2,4},{6,8},{10,12},{4,2},{8,6},{12,10},{3,5},{7,9},{11,13},{5,3},... | collective-permute-start | bytes 1572872 | tf_op jit(solution)/shard_map/ppermute | solution.py:302
  91.7 12.5 %collective-permute-start.18 = (bf16[2,128,1024]{2,1,0:T(8,128)(2,1)S(1)}, bf16[2,128,1024]{2,1,0:T(8,128)(2,1)S(1)}, u32[]{:S(2)}, u32[]{:S(2)}) collective-permute-start(bf16[2,128,1024]{2,1,0:T(8,128)(2,1)S(1)} %get-tuple-element.61), channel_id=1, source_target_pairs={{0,16},{32,48},{64,80},{96,112},{128,144},{160,176},{192,208},{224... | collective-permute-start | bytes 1572872 | tf_op jit(solution)/shard_map/ppermute | solution.py:302
  96.0 8.3 %collective-permute-start.19 = (bf16[2,128,1024]{2,1,0:T(8,128)(2,1)S(1)}, bf16[2,128,1024]{2,1,0:T(8,128)(2,1)S(1)}, u32[]{:S(2)}, u32[]{:S(2)}) collective-permute-start(bf16[2,128,1024]{2,1,0:T(8,128)(2,1)S(1)} %get-tuple-element.61), channel_id=1, source_target_pairs={{16,32},{48,64},{80,96},{112,128},{144,160},{176,192},{208,224},{3... | collective-permute-start | bytes 1572872 | tf_op jit(solution)/shard_map/ppermute | solution.py:302
  96.7 12.7 %collective-permute-start.20 = (bf16[2,128,1024]{2,1,0:T(8,128)(2,1)S(1)}, bf16[2,128,1024]{2,1,0:T(8,128)(2,1)S(1)}, u32[]{:S(2)}, u32[]{:S(2)}) collective-permute-start(bf16[2,128,1024]{2,1,0:T(8,128)(2,1)S(1)} %get-tuple-element.61), channel_id=1, source_target_pairs={{0,2},{4,6},{8,10},{12,14},{2,0},{6,4},{10,8},{14,12},{1,3},{5,7},... | collective-permute-start | bytes 1572872 | tf_op jit(solution)/shard_map/ppermute | solution.py:302
  101.6 7.8 %collective-permute-start.21 = (bf16[2,128,1024]{2,1,0:T(8,128)(2,1)S(1)}, bf16[2,128,1024]{2,1,0:T(8,128)(2,1)S(1)}, u32[]{:S(2)}, u32[]{:S(2)}) collective-permute-start(bf16[2,128,1024]{2,1,0:T(8,128)(2,1)S(1)} %get-tuple-element.61), channel_id=1, source_target_pairs={{2,4},{6,8},{10,12},{4,2},{8,6},{12,10},{3,5},{7,9},{11,13},{5,3},... | collective-permute-start | bytes 1572872 | tf_op jit(solution)/shard_map/ppermute | solution.py:302
